TPU v7x, 256 devices: a whole 4x4x8 slice. The times are simulated.
256 devices in a mesh: gx: 8 (over z), gy: 4 (over y_lo, core), gz: 8 (over y_hi, x).
Axes of the slice: x: 4, y: 4 (y_hi: 2, y_lo: 2; y = y_hi * 2 + y_lo), z: 8, core: 2. Of those that a mesh axis runs over, the one named last changes fastest.
Arguments:
- incident: bfloat16 [8, 4, 8, 2, 1280, 128], P('gx', 'gy', 'gz'), may hold values from -6 to 6
- response: bfloat16 [8, 4, 8, 2, 1280, 1280], P('gx', 'gy', 'gz'), may hold values from -0.125 to 0.125
- radiation: bfloat16 [8, 4, 8, 2, 512, 1280], P('gx', 'gy', 'gz'), may hold values from -0.0078125 to 0.0078125
- face_index: int32 [8, 4, 8, 6, 192], P('gx', 'gy', 'gz'), may hold values from 0 to 1279, as said below
- linked: int32 [8, 4, 8, 6], P('gx', 'gy', 'gz'), may hold values 0 or 1
Outputs:
- far_field: float32 [2, 128, 512], P(None, ('gx', 'gy'), 'gz')
Inputs may be any that keep to these rules, and one draw needn't show every extreme that they name: `face_index`: the 1152 entries of one subdomain are distinct.
All inputs are finite; a program needn't handle non-finite values. No bound on the sum of `linked` on one device may be relied on, other than what follows from the above.
Results may differ from a plain program's by a relative error of at most 0.004.
Values may be sent and summed in bfloat16 or wider, within the bound.
A program may use at most 64 MiB of HBM per device.

v0:
```python
import jax
import jax.numpy as jnp
from jax import lax
from jax.sharding import PartitionSpec as P

M = 1280
FACE = 192
ITERS = 2


def with_halo(cells, sides, width):
    for axis, dim in sides:
        count = lax.axis_size(axis)
        ends = count - 1
        head = lax.slice_in_dim(cells, 0, width, axis=dim)
        tail = lax.slice_in_dim(cells, cells.shape[dim] - width, cells.shape[dim], axis=dim)
        cells = jnp.concatenate(
            [
                lax.ppermute(tail, axis, [(i, (i + 1) % count) for i in range(ends)]),
                cells,
                lax.ppermute(head, axis, [((i + 1) % count, i) for i in range(ends)]),
            ],
            axis=dim,
        )
    return cells


def cut_along(value, dim, size):
    shape = value.shape
    pieces = value.reshape(*shape[:dim], size, shape[dim] // size, *shape[dim + 1 :])
    return jnp.moveaxis(pieces, dim, 0)


def summed_on_arrival(value, axis, dim):
    size = lax.axis_size(axis)
    pieces = lax.all_to_all(cut_along(value, dim, size), axis, 0, 0, tiled=True)
    return jnp.sum(pieces, axis=0)


def complex_dot(left_side, right_side):
    real_part = jnp.dot(left_side[0], right_side[0], preferred_element_type=jnp.float32) - jnp.dot(
        left_side[1], right_side[1], preferred_element_type=jnp.float32
    )
    imag_part = jnp.dot(left_side[0], right_side[1], preferred_element_type=jnp.float32) + jnp.dot(
        left_side[1], right_side[0], preferred_element_type=jnp.float32
    )
    return jnp.stack([real_part, imag_part])


def pick_rows(selector, values):
    picked = [
        jnp.dot(selector, values[part_pos], preferred_element_type=jnp.float32)
        for part_pos in range(2)
    ]
    return jnp.stack(picked).astype(jnp.bfloat16)


def put_rows(selector, values):
    placed = [
        lax.dot_general(
            selector, values[part_pos], (((0,), (0,)), ((), ())), preferred_element_type=jnp.float32
        )
        for part_pos in range(2)
    ]
    return jnp.stack(placed).astype(jnp.bfloat16)


def swap_faces(face_block, axis_pos):
    if axis_pos == 0:
        return with_halo(face_block, (("gx", 1),), 1)
    if axis_pos == 1:
        return with_halo(face_block, (("gy", 1),), 1)
    return with_halo(face_block, (("gz", 1),), 1)


def shards(incident, response, radiation, face_index, linked):
    source = incident[0, 0, 0]
    response_mat = response[0, 0, 0]
    radiation_mat = radiation[0, 0, 0]
    slots = face_index[0, 0, 0].reshape(-1)
    linked_faces = linked[0, 0, 0]
    columns = source.shape[-1]
    positions = lax.broadcasted_iota(jnp.int32, (slots.shape[0], M), 1)
    selector = (slots[:, None] == positions).astype(jnp.bfloat16)
    traces = jnp.zeros((2, M, columns), jnp.bfloat16)
    for sweep in range(ITERS):
        summed = (traces.astype(jnp.float32) + source.astype(jnp.float32)).astype(jnp.bfloat16)
        outgoing = complex_dot(response_mat, summed).astype(jnp.bfloat16)
        pieces = []
        for axis_pos in range(3):
            part_select = selector[2 * axis_pos * FACE : (2 * axis_pos + 2) * FACE]
            face_block = pick_rows(part_select, outgoing).reshape(2, 2, FACE, columns)
            arrived = swap_faces(face_block, axis_pos)
            pieces.append(arrived[:, 0])
            pieces.append(arrived[:, 3])
        incoming = jnp.stack(pieces, 1) * linked_faces[None, :, None, None].astype(jnp.bfloat16)
        traces = put_rows(selector, incoming.reshape(2, 6 * FACE, columns))
    currents = (traces.astype(jnp.float32) + source.astype(jnp.float32)).astype(jnp.bfloat16)
    contract = (((0,), (1,)), ((), ()))
    real_part = lax.dot_general(
        currents[0], radiation_mat[0], contract, preferred_element_type=jnp.float32
    ) - lax.dot_general(currents[1], radiation_mat[1], contract, preferred_element_type=jnp.float32)
    imag_part = lax.dot_general(
        currents[1], radiation_mat[0], contract, preferred_element_type=jnp.float32
    ) + lax.dot_general(currents[0], radiation_mat[1], contract, preferred_element_type=jnp.float32)
    radiated = jnp.stack([real_part, imag_part])
    partial_field = summed_on_arrival(radiated, "gz", 2)
    return summed_on_arrival(partial_field, ("gx", "gy"), 1)


def solution(mesh):
    return jax.shard_map(
        shards,
        mesh=mesh,
        in_specs=(
            P("gx", "gy", "gz", None, None, None),
            P("gx", "gy", "gz", None, None, None),
            P("gx", "gy", "gz", None, None, None),
            P("gx", "gy", "gz", None, None),
            P("gx", "gy", "gz", None),
        ),
        out_specs=P(None, ("gx", "gy"), "gz"),
        check_vma=False,
    )
```

profile of v0, /device:TPU:1, one launch (start us, length us, event | category | flops | bytes accessed | tf_op | source)
XLA Modules:
  0.0 121.4 jit_solution(14188138568112825521)
XLA Ops:
  0.0 3.1 %fusion.10 = f32[1280,128]{1,0:T(8,128)S(1)} fusion(bf16[1,1,1,2,1280,1280]{5,4,3,2,1,0:T(8,128)(2,1)} %param.6, bf16[1,1,1,2,1280,128]{5,4,3,2,1,0:T(8,128)(2,1)} %param.5), kind=kOutput, calls=%fused_computation.11 | convolution fusion | flops 419430400 | bytes 4259840 | tf_op jit(solution)/shard_map/dot_general | solution.py:41
  7.6 3.2 %fusion.56 = bf16[1280,128,1]{1,0,2:T(8,128)(2,1)S(1)} fusion(f32[1280,128]{1,0:T(8,128)S(1)} %fusion.10, bf16[1,1,1,2,1280,1280]{5,4,3,2,1,0:T(8,128)(2,1)} %param.6, bf16[1,1,1,2,1280,128]{5,4,3,2,1,0:T(8,128)(2,1)S(1)} %copy-done), kind=kOutput, calls=%fused_computation.41 | convolution fusion | flops 419758080 | bytes 4587520 | tf_op jit(solution)/shard_map/dot_general | solution.py:41
  12.8 4.4 %collective-permute-start = (bf16[2,1,192,128]{3,2,1,0:T(8,128)(2,1)S(1)}, bf16[2,1,192,128]{3,2,1,0:T(8,128)(2,1)S(1)}, u32[]{:S(2)}, u32[]{:S(2)}) collective-permute-start(bf16[2,1,192,128]{3,2,1,0:T(8,128)(2,1)S(1)} %get-tuple-element.23), channel_id=1, source_target_pairs={{0,32},{32,64},{64,96},{96,128},{128,160},{160,192},{192,224},{1,3... | collective-permute-start | bytes 294920 | tf_op jit(solution)/shard_map/ppermute | solution.py:19
  17.2 1.3 %collective-permute-start.1 = (bf16[2,1,192,128]{3,2,1,0:T(8,128)(2,1)S(1)}, bf16[2,1,192,128]{3,2,1,0:T(8,128)(2,1)S(1)}, u32[]{:S(2)}, u32[]{:S(2)}) collective-permute-start(bf16[2,1,192,128]{3,2,1,0:T(8,128)(2,1)S(1)} %get-tuple-element.22), channel_id=1, source_target_pairs={{32,0},{64,32},{96,64},{128,96},{160,128},{192,160},{224,192},{33,... | collective-permute-start | bytes 294920 | tf_op jit(solution)/shard_map/ppermute | solution.py:21
  19.4 4.0 %collective-permute-start.2 = (bf16[2,1,192,128]{3,2,1,0:T(8,128)(2,1)S(1)}, bf16[2,1,192,128]{3,2,1,0:T(8,128)(2,1)S(1)}, u32[]{:S(2)}, u32[]{:S(2)}) collective-permute-start(bf16[2,1,192,128]{3,2,1,0:T(8,128)(2,1)S(1)} %get-tuple-element.21), channel_id=1, source_target_pairs={{0,8},{8,16},{16,24},{1,9},{9,17},{17,25},{2,10},{10,18},{18,26},{... | collective-permute-start | bytes 294920 | tf_op jit(solution)/shard_map/ppermute | solution.py:19
  23.4 1.9 %collective-permute-start.3 = (bf16[2,1,192,128]{3,2,1,0:T(8,128)(2,1)S(1)}, bf16[2,1,192,128]{3,2,1,0:T(8,128)(2,1)S(1)}, u32[]{:S(2)}, u32[]{:S(2)}) collective-permute-start(bf16[2,1,192,128]{3,2,1,0:T(8,128)(2,1)S(1)} %get-tuple-element.20), channel_id=1, source_target_pairs={{8,0},{16,8},{24,16},{9,1},{17,9},{25,17},{10,2},{18,10},{26,18},{... | collective-permute-start | bytes 294920 | tf_op jit(solution)/shard_map/ppermute | solution.py:21
  26.2 3.1 %collective-permute-start.4 = (bf16[2,1,192,128]{3,2,1,0:T(8,128)(2,1)S(1)}, bf16[2,1,192,128]{3,2,1,0:T(8,128)(2,1)S(1)}, u32[]{:S(2)}, u32[]{:S(2)}) collective-permute-start(bf16[2,1,192,128]{3,2,1,0:T(8,128)(2,1)S(1)} %get-tuple-element.19), channel_id=1, source_target_pairs={{0,1},{1,2},{2,3},{3,4},{4,5},{5,6},{6,7},{8,9},{9,10},{10,11},{11... | collective-permute-start | bytes 294920 | tf_op jit(solution)/shard_map/ppermute | solution.py:19
  29.4 1.5 %collective-permute-start.5 = (bf16[2,1,192,128]{3,2,1,0:T(8,128)(2,1)S(1)}, bf16[2,1,192,128]{3,2,1,0:T(8,128)(2,1)S(1)}, u32[]{:S(2)}, u32[]{:S(2)}) collective-permute-start(bf16[2,1,192,128]{3,2,1,0:T(8,128)(2,1)S(1)} %get-tuple-element.18), channel_id=1, source_target_pairs={{1,0},{2,1},{3,2},{4,3},{5,4},{6,5},{7,6},{9,8},{10,9},{11,10},{12... | collective-permute-start | bytes 294920 | tf_op jit(solution)/shard_map/ppermute | solution.py:21
  31.0 3.7 %collective-permute-done.5 = bf16[2,1,192,128]{3,2,1,0:T(8,128)(2,1)S(1)} collective-permute-done((bf16[2,1,192,128]{3,2,1,0:T(8,128)(2,1)S(1)}, bf16[2,1,192,128]{3,2,1,0:T(8,128)(2,1)S(1)}, u32[]{:S(2)}, u32[]{:S(2)}) %collective-permute-start.5) | collective-permute-done | bytes 98336 | tf_op jit(solution)/shard_map/ppermute | solution.py:21
  34.9 1.9 %fusion.55 = bf16[1,1280,128]{2,1,0:T(8,128)(2,1)S(1)} fusion(bf16[1152,128]{1,0:T(8,128)(2,1)S(1)} %bitcast.187, s32[1152]{0:T(1024)S(1)} %eq.10), kind=kOutput, calls=%fused_computation.40 | convolution fusion | flops 379125760 | bytes 627200 | tf_op jit(solution)/shard_map/dot_general | solution.py:60
  36.8 1.9 %fusion.54 = bf16[1,1280,128]{2,1,0:T(8,128)(2,1)S(1)} fusion(bf16[1152,128]{1,0:T(8,128)(2,1)S(1)} %bitcast.186, s32[1152]{0:T(1024)S(1)} %eq.10), kind=kOutput, calls=%fused_computation.39 | convolution fusion | flops 379125760 | bytes 627200 | tf_op jit(solution)/shard_map/dot_general | solution.py:60
  46.4 3.1 %collective-permute-start.10 = (bf16[2,1,192,128]{3,2,1,0:T(8,128)(2,1)S(1)}, bf16[2,1,192,128]{3,2,1,0:T(8,128)(2,1)S(1)}, u32[]{:S(2)}, u32[]{:S(2)}) collective-permute-start(bf16[2,1,192,128]{3,2,1,0:T(8,128)(2,1)S(1)} %get-tuple-element.13), channel_id=1, source_target_pairs={{0,1},{1,2},{2,3},{3,4},{4,5},{5,6},{6,7},{8,9},{9,10},{10,11},{11... | collective-permute-start | bytes 294920 | tf_op jit(solution)/shard_map/ppermute | solution.py:19
  49.5 4.2 %collective-permute-start.6 = (bf16[2,1,192,128]{3,2,1,0:T(8,128)(2,1)S(1)}, bf16[2,1,192,128]{3,2,1,0:T(8,128)(2,1)S(1)}, u32[]{:S(2)}, u32[]{:S(2)}) collective-permute-start(bf16[2,1,192,128]{3,2,1,0:T(8,128)(2,1)S(1)} %get-tuple-element.17), channel_id=1, source_target_pairs={{0,32},{32,64},{64,96},{96,128},{128,160},{160,192},{192,224},{1,3... | collective-permute-start | bytes 294920 | tf_op jit(solution)/shard_map/ppermute | solution.py:19
  53.8 5.7 %collective-permute-start.8 = (bf16[2,1,192,128]{3,2,1,0:T(8,128)(2,1)S(1)}, bf16[2,1,192,128]{3,2,1,0:T(8,128)(2,1)S(1)}, u32[]{:S(2)}, u32[]{:S(2)}) collective-permute-start(bf16[2,1,192,128]{3,2,1,0:T(8,128)(2,1)S(1)} %get-tuple-element.15), channel_id=1, source_target_pairs={{0,8},{8,16},{16,24},{1,9},{9,17},{17,25},{2,10},{10,18},{18,26},{... | collective-permute-start | bytes 294920 | tf_op jit(solution)/shard_map/ppermute | solution.py:19
  59.4 1.3 %collective-permute-start.7 = (bf16[2,1,192,128]{3,2,1,0:T(8,128)(2,1)S(1)}, bf16[2,1,192,128]{3,2,1,0:T(8,128)(2,1)S(1)}, u32[]{:S(2)}, u32[]{:S(2)}) collective-permute-start(bf16[2,1,192,128]{3,2,1,0:T(8,128)(2,1)S(1)} %get-tuple-element.16), channel_id=1, source_target_pairs={{32,0},{64,32},{96,64},{128,96},{160,128},{192,160},{224,192},{33,... | collective-permute-start | bytes 294920 | tf_op jit(solution)/shard_map/ppermute | solution.py:21
  60.7 1.9 %collective-permute-start.9 = (bf16[2,1,192,128]{3,2,1,0:T(8,128)(2,1)S(1)}, bf16[2,1,192,128]{3,2,1,0:T(8,128)(2,1)S(1)}, u32[]{:S(2)}, u32[]{:S(2)}) collective-permute-start(bf16[2,1,192,128]{3,2,1,0:T(8,128)(2,1)S(1)} %get-tuple-element.14), channel_id=1, source_target_pairs={{8,0},{16,8},{24,16},{9,1},{17,9},{25,17},{10,2},{18,10},{26,18},{... | collective-permute-start | bytes 294920 | tf_op jit(solution)/shard_map/ppermute | solution.py:21
  62.7 1.5 %collective-permute-start.11 = (bf16[2,1,192,128]{3,2,1,0:T(8,128)(2,1)S(1)}, bf16[2,1,192,128]{3,2,1,0:T(8,128)(2,1)S(1)}, u32[]{:S(2)}, u32[]{:S(2)}) collective-permute-start(bf16[2,1,192,128]{3,2,1,0:T(8,128)(2,1)S(1)} %get-tuple-element.12), channel_id=1, source_target_pairs={{1,0},{2,1},{3,2},{4,3},{5,4},{6,5},{7,6},{9,8},{10,9},{11,10},{12... | collective-permute-start | bytes 294920 | tf_op jit(solution)/shard_map/ppermute | solution.py:21
  65.3 1.4 %collective-permute-done.9 = bf16[2,1,192,128]{3,2,1,0:T(8,128)(2,1)S(1)} collective-permute-done((bf16[2,1,192,128]{3,2,1,0:T(8,128)(2,1)S(1)}, bf16[2,1,192,128]{3,2,1,0:T(8,128)(2,1)S(1)}, u32[]{:S(2)}, u32[]{:S(2)}) %collective-permute-start.9) | collective-permute-done | bytes 98336 | tf_op jit(solution)/shard_map/ppermute | solution.py:21
  66.7 1.3 %collective-permute-done.11 = bf16[2,1,192,128]{3,2,1,0:T(8,128)(2,1)S(1)} collective-permute-done((bf16[2,1,192,128]{3,2,1,0:T(8,128)(2,1)S(1)}, bf16[2,1,192,128]{3,2,1,0:T(8,128)(2,1)S(1)}, u32[]{:S(2)}, u32[]{:S(2)}) %collective-permute-start.11) | collective-permute-done | bytes 98336 | tf_op jit(solution)/shard_map/ppermute | solution.py:21
  68.2 1.9 %fusion.53 = bf16[1,1280,128]{2,1,0:T(8,128)(2,1)S(1)} fusion(bf16[1152,128]{1,0:T(8,128)(2,1)S(1)} %bitcast.188, s32[1152]{0:T(1024)S(1)} %eq.10), kind=kOutput, calls=%fused_computation.38 | convolution fusion | flops 379125760 | bytes 627200 | tf_op jit(solution)/shard_map/dot_general | solution.py:60
  70.1 1.9 %fusion.52 = bf16[1,1280,128]{2,1,0:T(8,128)(2,1)S(1)} fusion(bf16[1152,128]{1,0:T(8,128)(2,1)S(1)} %bitcast.185, s32[1152]{0:T(1024)S(1)} %eq.10), kind=kOutput, calls=%fused_computation.37 | convolution fusion | flops 379125760 | bytes 627200 | tf_op jit(solution)/shard_map/dot_general | solution.py:60
  74.1 1.9 %fusion.89 = f32[128,512]{1,0:T(8,128)S(1)} fusion(f32[128,512]{1,0:T(8,128)S(1)} %fusion.78, bf16[1,1,1,2,512,1280]{5,4,3,2,1,0:T(8,128)(2,1)} %param.7, bf16[2,1280,128]{2,1,0:T(8,128)(2,1)S(1)} %fusion.77), kind=kOutput, calls=%fused_computation.66 | convolution fusion | flops 167837696 | bytes 2162688 | tf_op jit(solution)/shard_map/dot_general | solution.py:103
  76.2 20.8 %all_to_all.10 = f32[8,2,128,64]{2,3,1,0:T(8,128)S(1)} all-to-all(f32[8,2,128,64]{2,3,1,0:T(8,128)S(1)} %copy.15), channel_id=1, replica_groups=mesh['gx'=8,'gy'=4,'gz'=8] {'gz'}, dimensions={0} | all-to-all | bytes 1048576 | tf_op jit(solution)/shard_map/all_to_all | solution.py:36
  97.3 22.0 %all_to_all.11 = f32[32,1,512]{2,1,0:T(1,128)S(1)} all-to-all(f32[32,1,512]{2,1,0:T(1,128)S(1)} %reshape.151), channel_id=1, replica_groups=mesh['gx'=8,'gy'=4,'gz'=8] {'gx','gy'}, dimensions={0} | all-to-all | bytes 131072 | tf_op jit(solution)/shard_map/all_to_all | solution.py:36
  (86 shorter events, 21.8 us)
Async XLA Ops:
  0.0 3.1 %copy-start = (bf16[1,1,1,2,1280,128]{5,4,3,2,1,0:T(8,128)(2,1)S(1)}, bf16[1,1,1,2,1280,128]{5,4,3,2,1,0:T(8,128)(2,1)}, u32[]{:S(2)}) copy-start(bf16[1,1,1,2,1280,128]{5,4,3,2,1,0:T(8,128)(2,1)} %param.5) | copy-start | bytes 1966084
  0.0 4.2 %copy-start.2 = (bf16[1,1,1,2,1280,1280]{5,4,3,2,1,0:T(8,128)(2,1)S(1)}, bf16[1,1,1,2,1280,1280]{5,4,3,2,1,0:T(8,128)(2,1)}, u32[]{:S(2)}) copy-start(bf16[1,1,1,2,1280,1280]{5,4,3,2,1,0:T(8,128)(2,1)} %param.6) | copy-start | bytes 19660804
  4.2 1.0 copy-start.1
  6.6 4.2 %slice-start = ((s8[6553600]{0:T(1024)(128)(4,1)}), s8[4194304]{0:T(1024)(128)(4,1)S(1)}, s32[]{:S(2)}) async-start(s8[6553600]{0:T(1024)(128)(4,1)} %bitcast.189), calls=%async_computation.2 | async-start | bytes 8388608
  7.6 3.2 %slice-start.1 = ((s8[6553600]{0:T(1024)(128)(4,1)}), s8[2359296]{0:T(1024)(128)(4,1)S(1)}, s32[]{:S(2)}) async-start(s8[6553600]{0:T(1024)(128)(4,1)} %bitcast.189), calls=%async_computation.3 | async-start | bytes 4718592
  11.9 17.5 %copy-start.4 = (s32[1,1,1,6]{3,2,1,0:T(1,128)S(1)}, s32[1,1,1,6]{3,2,1,0:T(1,128)}, u32[]{:S(2)}) copy-start(s32[1,1,1,6]{3,2,1,0:T(1,128)} %param.9) | copy-start | bytes 76
  12.8 16.6 %collective-permute-start = (bf16[2,1,192,128]{3,2,1,0:T(8,128)(2,1)S(1)}, bf16[2,1,192,128]{3,2,1,0:T(8,128)(2,1)S(1)}, u32[]{:S(2)}, u32[]{:S(2)}) collective-permute-start(bf16[2,1,192,128]{3,2,1,0:T(8,128)(2,1)S(1)} %get-tuple-element.23), channel_id=1, source_target_pairs={{0,32},{32,64},{64,96},{96,128},{128,160},{160,192},{192,224},{1,3... | collective-permute-start | bytes 294920 | tf_op jit(solution)/shard_map/ppermute | solution.py:19
  17.2 13.7 %collective-permute-start.1 = (bf16[2,1,192,128]{3,2,1,0:T(8,128)(2,1)S(1)}, bf16[2,1,192,128]{3,2,1,0:T(8,128)(2,1)S(1)}, u32[]{:S(2)}, u32[]{:S(2)}) collective-permute-start(bf16[2,1,192,128]{3,2,1,0:T(8,128)(2,1)S(1)} %get-tuple-element.22), channel_id=1, source_target_pairs={{32,0},{64,32},{96,64},{128,96},{160,128},{192,160},{224,192},{33,... | collective-permute-start | bytes 294920 | tf_op jit(solution)/shard_map/ppermute | solution.py:21
  19.4 11.6 %collective-permute-start.2 = (bf16[2,1,192,128]{3,2,1,0:T(8,128)(2,1)S(1)}, bf16[2,1,192,128]{3,2,1,0:T(8,128)(2,1)S(1)}, u32[]{:S(2)}, u32[]{:S(2)}) collective-permute-start(bf16[2,1,192,128]{3,2,1,0:T(8,128)(2,1)S(1)} %get-tuple-element.21), channel_id=1, source_target_pairs={{0,8},{8,16},{16,24},{1,9},{9,17},{17,25},{2,10},{10,18},{18,26},{... | collective-permute-start | bytes 294920 | tf_op jit(solution)/shard_map/ppermute | solution.py:19
  23.4 7.5 %collective-permute-start.3 = (bf16[2,1,192,128]{3,2,1,0:T(8,128)(2,1)S(1)}, bf16[2,1,192,128]{3,2,1,0:T(8,128)(2,1)S(1)}, u32[]{:S(2)}, u32[]{:S(2)}) collective-permute-start(bf16[2,1,192,128]{3,2,1,0:T(8,128)(2,1)S(1)} %get-tuple-element.20), channel_id=1, source_target_pairs={{8,0},{16,8},{24,16},{9,1},{17,9},{25,17},{10,2},{18,10},{26,18},{... | collective-permute-start | bytes 294920 | tf_op jit(solution)/shard_map/ppermute | solution.py:21
  26.2 4.8 %collective-permute-start.4 = (bf16[2,1,192,128]{3,2,1,0:T(8,128)(2,1)S(1)}, bf16[2,1,192,128]{3,2,1,0:T(8,128)(2,1)S(1)}, u32[]{:S(2)}, u32[]{:S(2)}) collective-permute-start(bf16[2,1,192,128]{3,2,1,0:T(8,128)(2,1)S(1)} %get-tuple-element.19), channel_id=1, source_target_pairs={{0,1},{1,2},{2,3},{3,4},{4,5},{5,6},{6,7},{8,9},{9,10},{10,11},{11... | collective-permute-start | bytes 294920 | tf_op jit(solution)/shard_map/ppermute | solution.py:19
  29.4 5.4 %collective-permute-start.5 = (bf16[2,1,192,128]{3,2,1,0:T(8,128)(2,1)S(1)}, bf16[2,1,192,128]{3,2,1,0:T(8,128)(2,1)S(1)}, u32[]{:S(2)}, u32[]{:S(2)}) collective-permute-start(bf16[2,1,192,128]{3,2,1,0:T(8,128)(2,1)S(1)} %get-tuple-element.18), channel_id=1, source_target_pairs={{1,0},{2,1},{3,2},{4,3},{5,4},{6,5},{7,6},{9,8},{10,9},{11,10},{12... | collective-permute-start | bytes 294920 | tf_op jit(solution)/shard_map/ppermute | solution.py:21
  46.4 20.4 %collective-permute-start.10 = (bf16[2,1,192,128]{3,2,1,0:T(8,128)(2,1)S(1)}, bf16[2,1,192,128]{3,2,1,0:T(8,128)(2,1)S(1)}, u32[]{:S(2)}, u32[]{:S(2)}) collective-permute-start(bf16[2,1,192,128]{3,2,1,0:T(8,128)(2,1)S(1)} %get-tuple-element.13), channel_id=1, source_target_pairs={{0,1},{1,2},{2,3},{3,4},{4,5},{5,6},{6,7},{8,9},{9,10},{10,11},{11... | collective-permute-start | bytes 294920 | tf_op jit(solution)/shard_map/ppermute | solution.py:19
  49.5 13.2 %collective-permute-start.6 = (bf16[2,1,192,128]{3,2,1,0:T(8,128)(2,1)S(1)}, bf16[2,1,192,128]{3,2,1,0:T(8,128)(2,1)S(1)}, u32[]{:S(2)}, u32[]{:S(2)}) collective-permute-start(bf16[2,1,192,128]{3,2,1,0:T(8,128)(2,1)S(1)} %get-tuple-element.17), channel_id=1, source_target_pairs={{0,32},{32,64},{64,96},{96,128},{128,160},{160,192},{192,224},{1,3... | collective-permute-start | bytes 294920 | tf_op jit(solution)/shard_map/ppermute | solution.py:19
  53.8 11.4 %collective-permute-start.8 = (bf16[2,1,192,128]{3,2,1,0:T(8,128)(2,1)S(1)}, bf16[2,1,192,128]{3,2,1,0:T(8,128)(2,1)S(1)}, u32[]{:S(2)}, u32[]{:S(2)}) collective-permute-start(bf16[2,1,192,128]{3,2,1,0:T(8,128)(2,1)S(1)} %get-tuple-element.15), channel_id=1, source_target_pairs={{0,8},{8,16},{16,24},{1,9},{9,17},{17,25},{2,10},{10,18},{18,26},{... | collective-permute-start | bytes 294920 | tf_op jit(solution)/shard_map/ppermute | solution.py:19
  59.4 5.8 %collective-permute-start.7 = (bf16[2,1,192,128]{3,2,1,0:T(8,128)(2,1)S(1)}, bf16[2,1,192,128]{3,2,1,0:T(8,128)(2,1)S(1)}, u32[]{:S(2)}, u32[]{:S(2)}) collective-permute-start(bf16[2,1,192,128]{3,2,1,0:T(8,128)(2,1)S(1)} %get-tuple-element.16), channel_id=1, source_target_pairs={{32,0},{64,32},{96,64},{128,96},{160,128},{192,160},{224,192},{33,... | collective-permute-start | bytes 294920 | tf_op jit(solution)/shard_map/ppermute | solution.py:21
  60.7 5.9 %collective-permute-start.9 = (bf16[2,1,192,128]{3,2,1,0:T(8,128)(2,1)S(1)}, bf16[2,1,192,128]{3,2,1,0:T(8,128)(2,1)S(1)}, u32[]{:S(2)}, u32[]{:S(2)}) collective-permute-start(bf16[2,1,192,128]{3,2,1,0:T(8,128)(2,1)S(1)} %get-tuple-element.14), channel_id=1, source_target_pairs={{8,0},{16,8},{24,16},{9,1},{17,9},{25,17},{10,2},{18,10},{26,18},{... | collective-permute-start | bytes 294920 | tf_op jit(solution)/shard_map/ppermute | solution.py:21
  62.7 5.4 %collective-permute-start.11 = (bf16[2,1,192,128]{3,2,1,0:T(8,128)(2,1)S(1)}, bf16[2,1,192,128]{3,2,1,0:T(8,128)(2,1)S(1)}, u32[]{:S(2)}, u32[]{:S(2)}) collective-permute-start(bf16[2,1,192,128]{3,2,1,0:T(8,128)(2,1)S(1)} %get-tuple-element.12), channel_id=1, source_target_pairs={{1,0},{2,1},{3,2},{4,3},{5,4},{6,5},{7,6},{9,8},{10,9},{11,10},{12... | collective-permute-start | bytes 294920 | tf_op jit(solution)/shard_map/ppermute | solution.py:21
  70.1 2.1 %copy-start.3 = (bf16[1,1,1,2,512,1280]{5,4,3,2,1,0:T(8,128)(2,1)S(1)}, bf16[1,1,1,2,512,1280]{5,4,3,2,1,0:T(8,128)(2,1)}, u32[]{:S(2)}) copy-start(bf16[1,1,1,2,512,1280]{5,4,3,2,1,0:T(8,128)(2,1)} %param.7) | copy-start | bytes 7864324
where the time goes:
time: 122 us; the launch traced here: 121 us
  blocking collectives  42.8 us (35%)
  starting transfers between devices  34 us (28%)
  matrix products  29.4 us (24%)
  waiting for transfers between devices  7.47 us (6%)
  local copies, waits for them, and re-layouts  3.58 us (3%)
  other arithmetic  3.52 us (3%)
    all_to_all x2, blocking collectives, summed_on_arrival(): pieces = lax.all_to_all(cut_along(value, dim, size), axis, 0, 0, tiled=True)  42.8 us
    ppermute x6, starting transfers between devices, with_halo(): lax.ppermute(tail, axis, [(i, (i + 1) % count) for i in range(ends)])  24.6 us
    ppermute x6, starting transfers between devices, with_halo(): lax.ppermute(head, axis, [((i + 1) % count, i) for i in range(ends)])  9.41 us
    dot_general x4, matrix products, put_rows(): lax.dot_general(selector, values[part_pos], (((0,), (0,)), ((), ())), pre...  7.56 us
    ppermute x6, waiting for transfers between devices, with_halo(): lax.ppermute(head, axis, [((i + 1) % count, i) for i in range(ends)])  7.46 us
    dot_general x12, matrix products, pick_rows(): jnp.dot(selector, values[part_pos], preferred_element_type=jnp.float32)  5.1 us
    dot_general x2, matrix products, complex_dot(): jnp.dot(left_side[0], right_side[0], preferred_element_type=jnp.float32)  4.37 us
    dot_general x2, matrix products, complex_dot(): jnp.dot(left_side[1], right_side[1], preferred_element_type=jnp.float32)  4.31 us
  transfers between devices with their start and end apart: 12, of which 4 were waited for; matrix products, arithmetic and copies ran while one was open for 2% of the time, Pallas kernels for 0%

commit v1 on v0

v1 whole, which is shorter than its diff:
```python
import functools

import jax
import jax.numpy as jnp
from jax import lax
from jax.experimental import pallas as pl
from jax.experimental.pallas import tpu as pltpu
from jax.sharding import PartitionSpec as P

M = 1280
FACE = 192
ANG = 512
EXC = 128
PADDED = 256
CHUNKS = 5
ROWS = M // CHUNKS
PARTS = 4
PART_ROWS = ANG // PARTS
BLOCK = 64
MESH = pl.DeviceIdType.MESH
PICK_ORDER = (4, 5, 0, 1, 3, 2)
BF16, F32 = jnp.bfloat16, jnp.float32


def plane_order():
    steps = [(a, b, c) for a in range(2) for b in range(4) for c in range(2) if (a, b, c) != (0, 0, 0)]
    return sorted(steps, key=lambda s: -((2 if s[1] == 2 else s[1] % 2) + (1 if s[2] else 2 * s[0])))


def kernel(
    incident, response, radiation, face_index, linked, out_ref,
    inc, resp, rad, slots_raw, slots, link, select, place, weights, outgoing, sent, arrived, total,
    keep, half_out, half_in, plane_out, plane_in, line_out, line_in,
    load_sem, resp_sem, face_send, face_recv, half_send, half_recv, plane_send, plane_recv, line_send, line_recv,
):
    gx, gy, gz = lax.axis_index("gx"), lax.axis_index("gy"), lax.axis_index("gz")
    core, y_lo = gy % 2, gy // 2
    x, y_hi = gz % 4, gz // 4
    me_plane = gz * 2 + y_lo
    coords = (gx, gy, gz)
    sizes = (8, 4, 8)

    loads = [
        pltpu.make_async_copy(incident, inc, load_sem.at[0]),
        pltpu.make_async_copy(face_index, slots_raw, load_sem.at[1]),
        pltpu.make_async_copy(linked, link, load_sem.at[2]),
    ]
    for load in loads:
        load.start()
    resp_loads = []
    for c in range(CHUNKS):
        rows = pl.ds(c * ROWS, ROWS)
        pair = [
            pltpu.make_async_copy(response.at[p, rows], resp.at[rows, pl.ds(p * M, M)], resp_sem.at[c, p])
            for p in range(2)
        ]
        for load in pair:
            load.start()
        resp_loads.append(pair)
    rad_loads = [
        pltpu.make_async_copy(radiation.at[p], rad.at[:, pl.ds(p * M, M)], load_sem.at[3 + p]) for p in range(2)
    ]
    for load in rad_loads:
        load.start()

    arrived[...] = jnp.zeros_like(arrived)
    plane_in[...] = jnp.zeros_like(plane_in)
    line_in[...] = jnp.zeros_like(line_in)

    barrier = pltpu.get_barrier_semaphore()

    def greet(device):
        pl.semaphore_signal(barrier, inc=1, device_id=device, device_id_type=MESH)

    def plane_peer(step):
        dyh, dx, dyl = step
        peer_gz = ((y_hi + dyh) % 2) * 4 + (x + dx) % 4
        peer_lo = (y_lo + dyl) % 2
        return peer_gz * 2 + peer_lo, (gx, peer_lo * 2 + core, peer_gz)

    order = plane_order()
    partner = (gx, gy + 1 - 2 * core, gz)
    cross = (gx, 3 - gy, gz)
    middle = (gy + 1) // 2 == 1
    for step in order:
        greet(plane_peer(step)[1])
    for d in range(1, 8):
        greet(((gx + d) % 8, gy, gz))
    greet(partner)

    @pl.when(middle)
    def _():
        greet(cross)

    slots[...] = jnp.full(slots.shape, -1, jnp.int32)
    loads[1].wait()
    slots[0:6, 0:FACE] = slots_raw[...]
    columns = lax.broadcasted_iota(jnp.int32, (128, 128), 1).astype(F32)
    for f in PICK_ORDER:
        row = slots[f : f + 1, :].astype(F32)
        for half, count in ((0, 128), (1, 64)):
            wide = jnp.broadcast_to(row[:, half * 128 : (half + 1) * 128], (128, 128))
            tall = jnp.transpose(wide)[:count]
            for c in range(M // 128):
                hit = tall - float(c * 128) == columns[:count]
                select[f, half * 128 : half * 128 + count, c * 128 : (c + 1) * 128] = jnp.where(hit, 1.0, 0.0).astype(BF16)

    def set_weights(rows, real, imag):
        low = pl.ds(rows.start, rows.size)
        high = pl.ds(M + rows.start, rows.size)
        weights[low, 0:EXC] = real
        weights[low, EXC : 2 * EXC] = imag
        weights[high, 0:EXC] = -imag
        weights[high, EXC : 2 * EXC] = real

    loads[0].wait()
    for c in range(CHUNKS):
        rows = pl.ds(c * ROWS, ROWS)
        set_weights(rows, inc[0, rows], inc[1, rows])

    def respond(first):
        for c in range(CHUNKS):
            rows = pl.ds(c * ROWS, ROWS)
            if first:
                for load in resp_loads[c]:
                    load.wait()
            outgoing[rows] = jnp.dot(resp[rows], weights[...], preferred_element_type=F32).astype(BF16)

    def neighbour(f):
        axis, up = f // 2, f % 2
        place_of = coords[axis]
        there = place_of < sizes[axis] - 1 if up else place_of > 0
        to = tuple(v + (1 if up else -1) if a == axis else v for a, v in enumerate(coords))
        return there, to

    def face_copy(it, f):
        there, to = neighbour(f)
        landing = f + 1 - 2 * (f % 2)
        return there, pltpu.make_async_remote_copy(
            src_ref=sent.at[it, f],
            dst_ref=arrived.at[it, pl.ds(landing * PADDED, FACE)],
            send_sem=face_send.at[it, f],
            recv_sem=face_recv.at[it, landing],
            device_id=to,
            device_id_type=MESH,
        )

    def send_faces(it):
        for f in PICK_ORDER:
            sent[it, f] = jnp.dot(select[f], outgoing[...], preferred_element_type=F32).astype(BF16)
            there, copy = face_copy(it, f)

            @pl.when(there)
            def _():
                copy.start()

    def take_faces(it, faces):
        for f in faces:
            there, _ = neighbour(f)

            @pl.when(there)
            def _():
                pltpu.make_async_remote_copy(
                    src_ref=sent.at[it, f],
                    dst_ref=arrived.at[it, pl.ds(f * PADDED, FACE)],
                    send_sem=face_send.at[it, f],
                    recv_sem=face_recv.at[it, f],
                    device_id=neighbour(f)[1],
                    device_id_type=MESH,
                ).wait_recv()

    def add_traces(it):
        take_faces(it, (0, 1, 2, 3))
        near = 4 * PADDED
        for c in range(CHUNKS):
            rows = pl.ds(c * ROWS, ROWS)
            total[rows] = jnp.dot(place[rows, 0:near], arrived[it, 0:near], preferred_element_type=F32)
        take_faces(it, (4, 5))
        for c in range(CHUNKS):
            rows = pl.ds(c * ROWS, ROWS)
            trace = total[rows] + jnp.dot(
                place[rows, near : 6 * PADDED], arrived[it, near : 6 * PADDED], preferred_element_type=F32
            )
            real = (trace[:, 0:EXC] + inc[0, rows].astype(F32)).astype(BF16)
            imag = (trace[:, EXC : 2 * EXC] + inc[1, rows].astype(F32)).astype(BF16)
            set_weights(rows, real, imag)

    respond(True)
    pl.semaphore_wait(barrier, 15 + 7 + 1 + jnp.where(middle, 1, 0))
    send_faces(0)

    loads[2].wait()
    for f in range(6):
        row = jnp.where(link[0, f] > 0, slots[f : f + 1, :], -1)
        for c in range(CHUNKS):
            spots = lax.broadcasted_iota(jnp.int32, (ROWS, PADDED), 0) + c * ROWS
            place[c * ROWS : (c + 1) * ROWS, f * PADDED : (f + 1) * PADDED] = jnp.where(spots == row, 1.0, 0.0).astype(BF16)

    add_traces(0)
    respond(False)
    send_faces(1)
    add_traces(1)

    lanes = lax.broadcasted_iota(jnp.int32, (PART_ROWS, EXC), 1)
    odd_core = (lanes // 4) % 2
    for load in rad_loads:
        load.wait()
    half_copies = []
    for q in range(PARTS):
        rows = pl.ds(q * PART_ROWS, PART_ROWS)
        field = jnp.dot(rad[rows], weights[...], preferred_element_type=F32)
        real, imag = field[:, 0:EXC], field[:, EXC : 2 * EXC]
        zero = jnp.where(odd_core == 0, real, pltpu.roll(imag, 4, 1))
        one = jnp.where(odd_core == 0, pltpu.roll(real, EXC - 4, 1), imag)
        keep[rows] = jnp.where(core == 0, zero, one)
        half_out[rows] = jnp.where(core == 0, one, zero)
        copy = pltpu.make_async_remote_copy(
            src_ref=half_out.at[rows],
            dst_ref=half_in.at[rows],
            send_sem=half_send.at[q],
            recv_sem=half_recv.at[q],
            device_id=partner,
            device_id_type=MESH,
        )
        copy.start()
        half_copies.append(copy)

    small = lax.broadcasted_iota(jnp.int32, (BLOCK // 2, EXC), 1)
    odd_lo = (small // 8) % 2
    for q in range(PARTS):
        half_copies[q].wait_recv()
        for b in range(PART_ROWS // BLOCK):
            start = q * PART_ROWS + b * BLOCK
            first = pl.ds(start, BLOCK // 2)
            second = pl.ds(start + BLOCK // 2, BLOCK // 2)
            top = keep[first] + half_in[first]
            low = keep[second] + half_in[second]
            slot = (q * (PART_ROWS // BLOCK) + b) * 2
            plane_out[slot] = jnp.where(odd_lo == 0, top, pltpu.roll(low, 8, 1)).astype(BF16)
            plane_out[slot + 1] = jnp.where(odd_lo == 0, pltpu.roll(top, EXC - 8, 1), low).astype(BF16)

    plane_copies = []
    for n, step in enumerate(order):
        peer, device = plane_peer(step)
        copy = pltpu.make_async_remote_copy(
            src_ref=plane_out.at[peer],
            dst_ref=plane_in.at[me_plane],
            send_sem=plane_send.at[n],
            recv_sem=plane_recv.at[me_plane],
            device_id=device,
            device_id_type=MESH,
        )
        copy.start()
        plane_copies.append(copy)
    for s in range(16):

        @pl.when(s != me_plane)
        def _():
            pltpu.make_async_remote_copy(
                src_ref=plane_out.at[s],
                dst_ref=plane_in.at[s],
                send_sem=plane_send.at[0],
                recv_sem=plane_recv.at[s],
                device_id=partner,
                device_id_type=MESH,
            ).wait_recv()

    piece = plane_out[me_plane].astype(F32)
    for s in range(16):
        piece = piece + plane_in[s].astype(F32)
    tall = jnp.concatenate([piece, pltpu.roll(piece, EXC - 8, 1)], axis=0)
    turned = jnp.transpose(jnp.concatenate([tall, tall], axis=0))
    for d in range(8):
        line_out[d] = turned[d * 16 : d * 16 + 8]
    line_copies = []
    for d in (4, 3, 5, 2, 6, 1, 7):
        peer = (gx + d) % 8
        copy = pltpu.make_async_remote_copy(
            src_ref=line_out.at[peer],
            dst_ref=line_in.at[gx],
            send_sem=line_send.at[d],
            recv_sem=line_recv.at[gx],
            device_id=(peer, gy, gz),
            device_id_type=MESH,
        )
        copy.start()
        line_copies.append(copy)
    for s in range(8):

        @pl.when(s != gx)
        def _():
            pltpu.make_async_remote_copy(
                src_ref=line_out.at[s],
                dst_ref=line_in.at[s],
                send_sem=line_send.at[0],
                recv_sem=line_recv.at[s],
                device_id=partner,
                device_id_type=MESH,
            ).wait_recv()

    result = line_out[gx]
    for s in range(8):
        result = result + line_in[s]
    out_ref[0] = result[0:4, 0:BLOCK]
    out_ref[1] = result[4:8, 0:BLOCK]

    for it in range(2):
        for f in range(6):
            there, copy = face_copy(it, f)

            @pl.when(there)
            def _():
                copy.wait_send()

    for copy in half_copies + plane_copies + line_copies:
        copy.wait_send()


def shards(incident, response, radiation, face_index, linked):
    anywhere = pl.BlockSpec(memory_space=pl.ANY)
    dma = pltpu.SemaphoreType.DMA
    return pl.pallas_call(
        kernel,
        out_shape=jax.ShapeDtypeStruct((2, 4, BLOCK), F32),
        in_specs=[anywhere] * 5,
        out_specs=pl.BlockSpec(memory_space=pltpu.VMEM),
        scratch_shapes=[
            pltpu.VMEM((2, M, EXC), BF16),
            pltpu.VMEM((M, 2 * M), BF16),
            pltpu.VMEM((ANG, 2 * M), BF16),
            pltpu.VMEM((6, FACE), jnp.int32),
            pltpu.VMEM((8, PADDED), jnp.int32),
            pltpu.SMEM((1, 6), jnp.int32),
            pltpu.VMEM((6, FACE, M), BF16),
            pltpu.VMEM((M, 6 * PADDED), BF16),
            pltpu.VMEM((2 * M, 2 * EXC), BF16),
            pltpu.VMEM((M, 2 * EXC), BF16),
            pltpu.VMEM((2, 6, FACE, 2 * EXC), BF16),
            pltpu.VMEM((2, 6 * PADDED, 2 * EXC), BF16),
            pltpu.VMEM((M, 2 * EXC), F32),
            pltpu.VMEM((ANG, EXC), F32),
            pltpu.VMEM((ANG, EXC), F32),
            pltpu.VMEM((ANG, EXC), F32),
            pltpu.VMEM((16, BLOCK // 2, EXC), BF16),
            pltpu.VMEM((16, BLOCK // 2, EXC), BF16),
            pltpu.VMEM((8, 8, EXC), F32),
            pltpu.VMEM((8, 8, EXC), F32),
            dma((5,)),
            dma((CHUNKS, 2)),
            dma((2, 6)),
            dma((2, 6)),
            dma((PARTS,)),
            dma((PARTS,)),
            dma((16,)),
            dma((16,)),
            dma((8,)),
            dma((8,)),
        ],
        compiler_params=pltpu.CompilerParams(
            collective_id=0, has_side_effects=True, vmem_limit_bytes=60 * 1024 * 1024
        ),
        cost_estimate=pl.CostEstimate(flops=8_000_000_000, bytes_accessed=10_000_000, transcendentals=0),
        name="schwarz",
    )(
        incident.reshape(2, M, EXC),
        response.reshape(2, M, M),
        radiation.reshape(2, ANG, M),
        face_index.reshape(6, FACE),
        linked.reshape(1, 6),
    )


def solution(mesh):
    return jax.shard_map(
        shards,
        mesh=mesh,
        in_specs=(
            P("gx", "gy", "gz", None, None, None),
            P("gx", "gy", "gz", None, None, None),
            P("gx", "gy", "gz", None, None, None),
            P("gx", "gy", "gz", None, None),
            P("gx", "gy", "gz", None),
        ),
        out_specs=P(None, ("gx", "gy"), "gz"),
        check_vma=False,
    )
```

time: 122 us -> 47.1 us (0.39)
  Pallas kernels: 0 us -> 44.4 us
  blocking collectives: 42.8 us -> 0 us
  starting transfers between devices: 34 us -> 0 us
  matrix products: 29.4 us -> 0 us
  waiting for transfers between devices: 7.47 us -> 0 us
  other arithmetic: 3.52 us -> 0 us
    pallas_call x0 -> x1, Pallas kernels: none -> 44.4 us  [shards(): pl.pallas_call(kernel, out_shape=jax.ShapeDtypeStruct((2, 4, BLOCK), F32)...]
    all_to_all x2 -> x0, blocking collectives: 42.8 us -> none  [summed_on_arrival(): pieces = lax.all_to_all(cut_along(value, dim, size), axis, 0, 0, tiled=True)]
    ppermute x12 -> x0, starting transfers between devices: 34 us -> none  [the longest x6 24.6 us: with_halo(): lax.ppermute(tail, axis, [(i, (i + 1) % count) for i in range(ends)])]
    dot_general x28 -> x0, matrix products: 29.4 us -> none  [the longest x4 7.56 us: put_rows(): lax.dot_general(selector, values[part_pos], (((0,), (0,)), ((), ())), pre...]
    ppermute x12 -> x0, waiting for transfers between devices: 7.47 us -> none  [the longest x6 7.46 us: with_halo(): lax.ppermute(head, axis, [((i + 1) % count, i) for i in range(ends)])]
    eq x1 -> x0, other arithmetic: 1.28 us -> none  [shards(): selector = (slots[:, None] == positions).astype(jnp.bfloat16)]
    unnamed x26 -> x2, local copies, waits for them, and re-layouts: 1.47 us -> 2.55 us
  transfers between devices with their start and end apart: 12 -> 0, of which waited for: 4 -> 0; matrix products, arithmetic and copies ran while one was open for 2% -> 0% of each run, Pallas kernels for 0% -> 0%
where the time goes in v1:
time: 47.1 us; the launch traced here: 47 us
  Pallas kernels  44.4 us (94%)
  local copies, waits for them, and re-layouts  2.55 us (5%)
    pallas_call x1, Pallas kernels, shards(): pl.pallas_call(kernel, out_shape=jax.ShapeDtypeStruct((2, 4, BLOCK), F32)...  44.4 us
    unnamed x2, local copies, waits for them, and re-layouts  2.55 us

profile of v1, /device:TPU:1, one launch (start us, length us, event | category | flops | bytes accessed | tf_op | source)
XLA Modules:
  0.0 47.0 jit_solution(747943653249085906)
XLA Ops:
  0.0 1.3 %copy.8 = s32[1,1,1,6,192]{4,3,2,1,0:T(8,128)} copy(s32[1,1,1,6,192]{4,2,3,1,0:T(1,128)} %param.8) | data formatting | bytes 9216
  1.3 44.4 %schwarz.1 = f32[2,4,64]{2,1,0:T(4,128)} custom-call(bf16[2,1280,128]{2,1,0:T(8,128)(2,1)} %bitcast.10, bf16[2,1280,1280]{2,1,0:T(8,128)(2,1)} %bitcast.8, bf16[2,512,1280]{2,1,0:T(8,128)(2,1)} %bitcast.9, s32[6,192]{1,0:T(8,128)} %bitcast.7, s32[1,6]{1,0:T(1,128)} %bitcast.11), custom_call_target="tpu_custom_call" | custom-call | flops 8000000000 | bytes 10000000 | tf_op jit(solution)/shard_map/schwarz/pallas_call | solution.py:322
  45.7 1.3 %copy.10 = f32[2,4,64]{2,1,0:T(4,128)} copy(f32[2,4,64]{2,1,0:T(4,128)} %schwarz.1) | data formatting | bytes 4096

commit v2 on v1

--- a/solution.py
+++ b/solution.py
@@ -18,7 +18,8 @@
 PART_ROWS = ANG // PARTS
 BLOCK = 64
 MESH = pl.DeviceIdType.MESH
-PICK_ORDER = (4, 5, 0, 1, 3, 2)
+PICK_ORDER = (4, 0, 1, 2, 3, 5)
+TAKE_ORDER = (2, 0, 1)
 BF16, F32 = jnp.bfloat16, jnp.float32
 
 
@@ -29,20 +30,13 @@
 
 def kernel(
     incident, response, radiation, face_index, linked, out_ref,
-    inc, resp, rad, slots_raw, slots, link, select, place, weights, outgoing, sent, arrived, total,
+    inc, resp, rad, slots_raw, slots, link, select, place, weights, outgoing, sent, near_in, far_in, total, columns, field,
     keep, half_out, half_in, plane_out, plane_in, line_out, line_in,
     load_sem, resp_sem, face_send, face_recv, half_send, half_recv, plane_send, plane_recv, line_send, line_recv,
 ):
-    gx, gy, gz = lax.axis_index("gx"), lax.axis_index("gy"), lax.axis_index("gz")
-    core, y_lo = gy % 2, gy // 2
-    x, y_hi = gz % 4, gz // 4
-    me_plane = gz * 2 + y_lo
-    coords = (gx, gy, gz)
-    sizes = (8, 4, 8)
-
     loads = [
-        pltpu.make_async_copy(incident, inc, load_sem.at[0]),
-        pltpu.make_async_copy(face_index, slots_raw, load_sem.at[1]),
+        pltpu.make_async_copy(face_index, slots_raw, load_sem.at[0]),
+        pltpu.make_async_copy(incident, inc, load_sem.at[1]),
         pltpu.make_async_copy(linked, link, load_sem.at[2]),
     ]
     for load in loads:
@@ -60,10 +54,15 @@
     rad_loads = [
         pltpu.make_async_copy(radiation.at[p], rad.at[:, pl.ds(p * M, M)], load_sem.at[3 + p]) for p in range(2)
     ]
-    for load in rad_loads:
-        load.start()
-
-    arrived[...] = jnp.zeros_like(arrived)
+
+    gx, gy, gz = lax.axis_index("gx"), lax.axis_index("gy"), lax.axis_index("gz")
+    core, y_lo = gy % 2, gy // 2
+    x, y_hi = gz % 4, gz // 4
+    me_plane = gz * 2 + y_lo
+
+    near_in[...] = jnp.zeros_like(near_in)
+    for g in range(3):
+        far_in[g, 0 : 2 * PADDED] = jnp.zeros((2 * PADDED, 2 * EXC), BF16)
     plane_in[...] = jnp.zeros_like(plane_in)
     line_in[...] = jnp.zeros_like(line_in)
 
@@ -92,18 +91,39 @@
     def _():
         greet(cross)
 
+    ahead, across = core, 1 - core
+    face_of = (4 * ahead, 4 * ahead + 1, 4 * across, 4 * across + 1, 2 + core, 3 - core)
+    place_a, place_b = gx * across + gz * ahead, gx * ahead + gz * across
+    there = (place_a > 0, place_a < 7, place_b > 0, place_b < 7, middle, None)
+    target = (
+        (gx - across, gy, gz - ahead),
+        (gx + across, gy, gz + ahead),
+        (gx - ahead, gy, gz - across),
+        (gx + ahead, gy, gz + across),
+        cross,
+        partner,
+    )
+    landing = (1, 0, 3, 2, 4, 5)
+
+    def guarded(role, action):
+        if there[role] is None:
+            action()
+        else:
+            pl.when(there[role])(action)
+
     slots[...] = jnp.full(slots.shape, -1, jnp.int32)
-    loads[1].wait()
-    slots[0:6, 0:FACE] = slots_raw[...]
-    columns = lax.broadcasted_iota(jnp.int32, (128, 128), 1).astype(F32)
-    for f in PICK_ORDER:
-        row = slots[f : f + 1, :].astype(F32)
+    loads[0].wait()
+    for f in range(6):
+        slots[f : f + 1, 0:FACE] = slots_raw[f]
+    lanes128 = lax.broadcasted_iota(jnp.int32, (128, 128), 1).astype(F32)
+    for r in PICK_ORDER:
+        row = slots[pl.ds(face_of[r], 1), :].astype(F32)
         for half, count in ((0, 128), (1, 64)):
             wide = jnp.broadcast_to(row[:, half * 128 : (half + 1) * 128], (128, 128))
             tall = jnp.transpose(wide)[:count]
             for c in range(M // 128):
-                hit = tall - float(c * 128) == columns[:count]
-                select[f, half * 128 : half * 128 + count, c * 128 : (c + 1) * 128] = jnp.where(hit, 1.0, 0.0).astype(BF16)
+                hit = tall - float(c * 128) == lanes128[:count]
+                select[r, half * 128 : half * 128 + count, c * 128 : (c + 1) * 128] = jnp.where(hit, 1.0, 0.0).astype(BF16)
 
     def set_weights(rows, real, imag):
         low = pl.ds(rows.start, rows.size)
@@ -113,7 +133,7 @@
         weights[high, 0:EXC] = -imag
         weights[high, EXC : 2 * EXC] = real
 
-    loads[0].wait()
+    loads[1].wait()
     for c in range(CHUNKS):
         rows = pl.ds(c * ROWS, ROWS)
         set_weights(rows, inc[0, rows], inc[1, rows])
@@ -124,106 +144,109 @@
             if first:
                 for load in resp_loads[c]:
                     load.wait()
+                if c == CHUNKS - 2:
+                    for load in rad_loads:
+                        load.start()
             outgoing[rows] = jnp.dot(resp[rows], weights[...], preferred_element_type=F32).astype(BF16)
 
-    def neighbour(f):
-        axis, up = f // 2, f % 2
-        place_of = coords[axis]
-        there = place_of < sizes[axis] - 1 if up else place_of > 0
-        to = tuple(v + (1 if up else -1) if a == axis else v for a, v in enumerate(coords))
-        return there, to
-
-    def face_copy(it, f):
-        there, to = neighbour(f)
-        landing = f + 1 - 2 * (f % 2)
-        return there, pltpu.make_async_remote_copy(
-            src_ref=sent.at[it, f],
-            dst_ref=arrived.at[it, pl.ds(landing * PADDED, FACE)],
-            send_sem=face_send.at[it, f],
-            recv_sem=face_recv.at[it, landing],
-            device_id=to,
+    def face_copy(it, role, to=None):
+        spot = landing[role] if to is None else to
+        if it == 0:
+            dst = near_in.at[pl.ds(spot * PADDED, FACE)]
+        else:
+            dst = far_in.at[spot // 2, pl.ds((spot % 2) * PADDED, FACE)]
+        return pltpu.make_async_remote_copy(
+            src_ref=sent.at[it, role],
+            dst_ref=dst,
+            send_sem=face_send.at[it, role],
+            recv_sem=face_recv.at[it, spot],
+            device_id=target[role],
             device_id_type=MESH,
         )
 
     def send_faces(it):
-        for f in PICK_ORDER:
-            sent[it, f] = jnp.dot(select[f], outgoing[...], preferred_element_type=F32).astype(BF16)
-            there, copy = face_copy(it, f)
-
-            @pl.when(there)
-            def _():
-                copy.start()
-
-    def take_faces(it, faces):
-        for f in faces:
-            there, _ = neighbour(f)
-
-            @pl.when(there)
-            def _():
-                pltpu.make_async_remote_copy(
-                    src_ref=sent.at[it, f],
-                    dst_ref=arrived.at[it, pl.ds(f * PADDED, FACE)],
-                    send_sem=face_send.at[it, f],
-                    recv_sem=face_recv.at[it, f],
-                    device_id=neighbour(f)[1],
-                    device_id_type=MESH,
-                ).wait_recv()
-
-    def add_traces(it):
-        take_faces(it, (0, 1, 2, 3))
-        near = 4 * PADDED
-        for c in range(CHUNKS):
-            rows = pl.ds(c * ROWS, ROWS)
-            total[rows] = jnp.dot(place[rows, 0:near], arrived[it, 0:near], preferred_element_type=F32)
-        take_faces(it, (4, 5))
-        for c in range(CHUNKS):
-            rows = pl.ds(c * ROWS, ROWS)
-            trace = total[rows] + jnp.dot(
-                place[rows, near : 6 * PADDED], arrived[it, near : 6 * PADDED], preferred_element_type=F32
-            )
-            real = (trace[:, 0:EXC] + inc[0, rows].astype(F32)).astype(BF16)
-            imag = (trace[:, EXC : 2 * EXC] + inc[1, rows].astype(F32)).astype(BF16)
-            set_weights(rows, real, imag)
+        for r in PICK_ORDER:
+            sent[it, r] = jnp.dot(select[r], outgoing[...], preferred_element_type=F32).astype(BF16)
+            guarded(r, face_copy(it, r).start)
+
+    def take_faces(it, roles):
+        for r in roles:
+            guarded(r, face_copy(it, r, r).wait_recv)
+
+    def add_traces():
+        for n, g in enumerate(TAKE_ORDER):
+            take_faces(0, (2 * g, 2 * g + 1))
+            span = slice(2 * g * PADDED, (2 * g + 2) * PADDED)
+            for c in range(CHUNKS):
+                rows = pl.ds(c * ROWS, ROWS)
+                trace = jnp.dot(place[rows, span], near_in[span], preferred_element_type=F32)
+                if n > 0:
+                    trace = trace + total[rows]
+                if n < 2:
+                    total[rows] = trace
+                else:
+                    real = (trace[:, 0:EXC] + inc[0, rows].astype(F32)).astype(BF16)
+                    imag = (trace[:, EXC : 2 * EXC] + inc[1, rows].astype(F32)).astype(BF16)
+                    set_weights(rows, real, imag)
+
+    def gather_columns(g, p):
+        picked = jnp.dot(
+            rad[:, p * M : (p + 1) * M], place[:, 2 * g * PADDED : (2 * g + 2) * PADDED], preferred_element_type=F32
+        )
+        columns[g, :, 2 * p * PADDED : (2 * p + 2) * PADDED] = picked.astype(BF16)
 
     respond(True)
     pl.semaphore_wait(barrier, 15 + 7 + 1 + jnp.where(middle, 1, 0))
     send_faces(0)
 
+    for load in rad_loads:
+        load.wait()
+    field[...] = jnp.dot(rad[...], weights[...], preferred_element_type=F32)
     loads[2].wait()
-    for f in range(6):
-        row = jnp.where(link[0, f] > 0, slots[f : f + 1, :], -1)
+    for r in range(6):
+        row = jnp.where(link[0, face_of[r]] > 0, slots[pl.ds(face_of[r], 1), :], -1)
         for c in range(CHUNKS):
             spots = lax.broadcasted_iota(jnp.int32, (ROWS, PADDED), 0) + c * ROWS
-            place[c * ROWS : (c + 1) * ROWS, f * PADDED : (f + 1) * PADDED] = jnp.where(spots == row, 1.0, 0.0).astype(BF16)
-
-    add_traces(0)
+            place[c * ROWS : (c + 1) * ROWS, r * PADDED : (r + 1) * PADDED] = jnp.where(spots == row, 1.0, 0.0).astype(BF16)
+    gather_columns(TAKE_ORDER[0], 0)
+    gather_columns(TAKE_ORDER[0], 1)
+
+    add_traces()
     respond(False)
     send_faces(1)
-    add_traces(1)
+    for g in TAKE_ORDER[1:]:
+        gather_columns(g, 0)
+        gather_columns(g, 1)
 
     lanes = lax.broadcasted_iota(jnp.int32, (PART_ROWS, EXC), 1)
     odd_core = (lanes // 4) % 2
-    for load in rad_loads:
-        load.wait()
     half_copies = []
-    for q in range(PARTS):
-        rows = pl.ds(q * PART_ROWS, PART_ROWS)
-        field = jnp.dot(rad[rows], weights[...], preferred_element_type=F32)
-        real, imag = field[:, 0:EXC], field[:, EXC : 2 * EXC]
-        zero = jnp.where(odd_core == 0, real, pltpu.roll(imag, 4, 1))
-        one = jnp.where(odd_core == 0, pltpu.roll(real, EXC - 4, 1), imag)
-        keep[rows] = jnp.where(core == 0, zero, one)
-        half_out[rows] = jnp.where(core == 0, one, zero)
-        copy = pltpu.make_async_remote_copy(
-            src_ref=half_out.at[rows],
-            dst_ref=half_in.at[rows],
-            send_sem=half_send.at[q],
-            recv_sem=half_recv.at[q],
-            device_id=partner,
-            device_id_type=MESH,
-        )
-        copy.start()
-        half_copies.append(copy)
+    for n, g in enumerate(TAKE_ORDER):
+        take_faces(1, (2 * g, 2 * g + 1))
+        low, high = slice(0, 2 * PADDED), slice(2 * PADDED, 4 * PADDED)
+        far_in[g, high, 0:EXC] = -far_in[g, low, EXC : 2 * EXC]
+        far_in[g, high, EXC : 2 * EXC] = far_in[g, low, 0:EXC]
+        for q in range(PARTS):
+            rows = pl.ds(q * PART_ROWS, PART_ROWS)
+            value = field[rows] + jnp.dot(columns[g, rows], far_in[g], preferred_element_type=F32)
+            if n < 2:
+                field[rows] = value
+                continue
+            real, imag = value[:, 0:EXC], value[:, EXC : 2 * EXC]
+            zero = jnp.where(odd_core == 0, real, pltpu.roll(imag, 4, 1))
+            one = jnp.where(odd_core == 0, pltpu.roll(real, EXC - 4, 1), imag)
+            keep[rows] = jnp.where(core == 0, zero, one)
+            half_out[rows] = jnp.where(core == 0, one, zero)
+            copy = pltpu.make_async_remote_copy(
+                src_ref=half_out.at[rows],
+                dst_ref=half_in.at[rows],
+                send_sem=half_send.at[q],
+                recv_sem=half_recv.at[q],
+                device_id=partner,
+                device_id_type=MESH,
+            )
+            copy.start()
+            half_copies.append(copy)
 
     small = lax.broadcasted_iota(jnp.int32, (BLOCK // 2, EXC), 1)
     odd_lo = (small // 8) % 2
@@ -285,6 +308,13 @@
         )
         copy.start()
         line_copies.append(copy)
+
+    for it in range(2):
+        for r in range(6):
+            guarded(r, face_copy(it, r).wait_send)
+    for copy in half_copies + plane_copies:
+        copy.wait_send()
+
     for s in range(8):
 
         @pl.when(s != gx)
@@ -303,16 +333,7 @@
         result = result + line_in[s]
     out_ref[0] = result[0:4, 0:BLOCK]
     out_ref[1] = result[4:8, 0:BLOCK]
-
-    for it in range(2):
-        for f in range(6):
-            there, copy = face_copy(it, f)
-
-            @pl.when(there)
-            def _():
-                copy.wait_send()
-
-    for copy in half_copies + plane_copies + line_copies:
+    for copy in line_copies:
         copy.wait_send()
 
 
@@ -321,14 +342,14 @@
     dma = pltpu.SemaphoreType.DMA
     return pl.pallas_call(
         kernel,
-        out_shape=jax.ShapeDtypeStruct((2, 4, BLOCK), F32),
+        out_shape=pltpu.VMEM((2, 4, BLOCK), F32),
         in_specs=[anywhere] * 5,
         out_specs=pl.BlockSpec(memory_space=pltpu.VMEM),
         scratch_shapes=[
             pltpu.VMEM((2, M, EXC), BF16),
             pltpu.VMEM((M, 2 * M), BF16),
             pltpu.VMEM((ANG, 2 * M), BF16),
-            pltpu.VMEM((6, FACE), jnp.int32),
+            pltpu.VMEM((6, 1, FACE), jnp.int32),
             pltpu.VMEM((8, PADDED), jnp.int32),
             pltpu.SMEM((1, 6), jnp.int32),
             pltpu.VMEM((6, FACE, M), BF16),
@@ -336,8 +357,11 @@
             pltpu.VMEM((2 * M, 2 * EXC), BF16),
             pltpu.VMEM((M, 2 * EXC), BF16),
             pltpu.VMEM((2, 6, FACE, 2 * EXC), BF16),
-            pltpu.VMEM((2, 6 * PADDED, 2 * EXC), BF16),
+            pltpu.VMEM((6 * PADDED, 2 * EXC), BF16),
+            pltpu.VMEM((3, 4 * PADDED, 2 * EXC), BF16),
             pltpu.VMEM((M, 2 * EXC), F32),
+            pltpu.VMEM((3, ANG, 4 * PADDED), BF16),
+            pltpu.VMEM((ANG, 2 * EXC), F32),
             pltpu.VMEM((ANG, EXC), F32),
             pltpu.VMEM((ANG, EXC), F32),
             pltpu.VMEM((ANG, EXC), F32),
@@ -365,7 +389,7 @@
         incident.reshape(2, M, EXC),
         response.reshape(2, M, M),
         radiation.reshape(2, ANG, M),
-        face_index.reshape(6, FACE),
+        face_index.reshape(6, 1, FACE),
         linked.reshape(1, 6),
     )
 

time: 47.1 us -> 43.4 us (0.921)
  local copies, waits for them, and re-layouts: 2.55 us -> 0.6 us
  Pallas kernels: 44.4 us -> 42.7 us
    unnamed x2 -> x1, local copies, waits for them, and re-layouts: 2.55 us -> 0.6 us
    pallas_call x1, Pallas kernels: 44.4 us -> 42.7 us  [shards(): pl.pallas_call(kernel, out_shape=pltpu.VMEM((2, 4, BLOCK), F32), in_specs...]
where the time goes in v2:
time: 43.4 us; the launch traced here: 43.3 us
  Pallas kernels  42.7 us (98%)
  local copies, waits for them, and re-layouts  0.6 us (1%)
    pallas_call x1, Pallas kernels, shards(): pl.pallas_call(kernel, out_shape=pltpu.VMEM((2, 4, BLOCK), F32), in_specs...  42.7 us

profile of v2, /device:TPU:1, one launch (start us, length us, event | category | flops | bytes accessed | tf_op | source)
XLA Modules:
  0.0 43.3 jit_solution(1729694673826768902)
XLA Ops:
  0.0 42.7 %schwarz.1 = f32[2,4,64]{2,1,0:T(4,128)S(1)} custom-call(bf16[2,1280,128]{2,1,0:T(8,128)(2,1)} %bitcast.7, bf16[2,1280,1280]{2,1,0:T(8,128)(2,1)} %bitcast.5, bf16[2,512,1280]{2,1,0:T(8,128)(2,1)} %bitcast.6, s32[6,1,192]{2,1,0:T(1,128)} %bitcast.8, s32[1,6]{1,0:T(1,128)} %bitcast.9), custom_call_target="tpu_custom_call" | custom-call | flops 8000000000 | bytes 10000000 | tf_op jit(solution)/shard_map/schwarz/pallas_call | solution.py:343
  42.7 0.6 %copy.7 = f32[2,4,64]{2,1,0:T(4,128)} copy(f32[2,4,64]{2,1,0:T(4,128)S(1)} %schwarz.1) | data formatting | bytes 4096

commit v3 on v2

--- a/solution.py
+++ b/solution.py
@@ -48,9 +48,14 @@
             pltpu.make_async_copy(response.at[p, rows], resp.at[rows, pl.ds(p * M, M)], resp_sem.at[c, p])
             for p in range(2)
         ]
-        for load in pair:
+        resp_loads.append(pair)
+
+    def start_response(c):
+        for load in resp_loads[c]:
             load.start()
-        resp_loads.append(pair)
+
+    start_response(0)
+    start_response(1)
     rad_loads = [
         pltpu.make_async_copy(radiation.at[p], rad.at[:, pl.ds(p * M, M)], load_sem.at[3 + p]) for p in range(2)
     ]
@@ -133,6 +138,7 @@
         weights[high, 0:EXC] = -imag
         weights[high, EXC : 2 * EXC] = real
 
+    start_response(2)
     loads[1].wait()
     for c in range(CHUNKS):
         rows = pl.ds(c * ROWS, ROWS)
@@ -144,34 +150,55 @@
             if first:
                 for load in resp_loads[c]:
                     load.wait()
-                if c == CHUNKS - 2:
+                if c + 3 < CHUNKS:
+                    start_response(c + 3)
+                if c + 3 == CHUNKS:
                     for load in rad_loads:
                         load.start()
             outgoing[rows] = jnp.dot(resp[rows], weights[...], preferred_element_type=F32).astype(BF16)
 
-    def face_copy(it, role, to=None):
-        spot = landing[role] if to is None else to
+    def into(it, spot):
         if it == 0:
-            dst = near_in.at[pl.ds(spot * PADDED, FACE)]
-        else:
-            dst = far_in.at[spot // 2, pl.ds((spot % 2) * PADDED, FACE)]
+            return near_in.at[pl.ds(spot * PADDED, FACE)]
+        return far_in.at[spot // 2, pl.ds((spot % 2) * PADDED, FACE)]
+
+    def face_copy(it, role, spot, device):
         return pltpu.make_async_remote_copy(
             src_ref=sent.at[it, role],
-            dst_ref=dst,
+            dst_ref=into(it, spot),
             send_sem=face_send.at[it, role],
             recv_sem=face_recv.at[it, spot],
-            device_id=target[role],
+            device_id=device,
             device_id_type=MESH,
         )
 
+    crossing = jnp.where((gz == 3) | (gz == 4), 1, 0)
+    far = 2 * across + jnp.where(gz == 3, 1, 0)
+    sequence = [
+        usual + crossing * (other - usual)
+        for usual, other in zip(PICK_ORDER, (far, 4, (far + 1) % 4, (far + 2) % 4, (far + 3) % 4))
+    ]
+
     def send_faces(it):
-        for r in PICK_ORDER:
+        for r in sequence:
             sent[it, r] = jnp.dot(select[r], outgoing[...], preferred_element_type=F32).astype(BF16)
-            guarded(r, face_copy(it, r).start)
+            line = jnp.where(r < 4, 1, 0)
+            up = r % 2
+            along_z = (r // 2 + core + 1) % 2 * line
+            along_x = (r // 2 + core) % 2 * line
+            move = 2 * up - 1
+            device = (gx + along_z * move, gy + (1 - line) * (3 - 2 * gy), gz + along_x * move)
+            at = gx * along_z + gz * along_x
+            last = 7 * up
+            inside = ((r < 4) & (at != last)) | ((r == 4) & middle)
+            spot = r + line * (1 - 2 * up)
+            pl.when(inside)(face_copy(it, r, spot, device).start)
+        sent[it, 5] = jnp.dot(select[5], outgoing[...], preferred_element_type=F32).astype(BF16)
+        face_copy(it, 5, 5, partner).start()
 
     def take_faces(it, roles):
         for r in roles:
-            guarded(r, face_copy(it, r, r).wait_recv)
+            guarded(r, face_copy(it, r, r, target[r]).wait_recv)
 
     def add_traces():
         for n, g in enumerate(TAKE_ORDER):
@@ -311,7 +338,7 @@
 
     for it in range(2):
         for r in range(6):
-            guarded(r, face_copy(it, r).wait_send)
+            guarded(r, face_copy(it, r, landing[r], target[r]).wait_send)
     for copy in half_copies + plane_copies:
         copy.wait_send()
 

time: 43.4 us -> 42.4 us (0.977)
  Pallas kernels: 42.7 us -> 41.8 us
    pallas_call x1, Pallas kernels: 42.7 us -> 41.8 us  [shards(): pl.pallas_call(kernel, out_shape=pltpu.VMEM((2, 4, BLOCK), F32), in_specs...]
where the time goes in v3:
time: 42.4 us
  Pallas kernels  41.8 us (99%)
  local copies, waits for them, and re-layouts  0.6 us (1%)
    pallas_call x1, Pallas kernels, shards(): pl.pallas_call(kernel, out_shape=pltpu.VMEM((2, 4, BLOCK), F32), in_specs...  41.8 us

profile of v3, /device:TPU:1, one launch (start us, length us, event | category | flops | bytes accessed | tf_op | source)
XLA Modules:
  0.0 42.4 jit_solution(4494816666228044761)
XLA Ops:
  0.0 41.8 %schwarz.1 = f32[2,4,64]{2,1,0:T(4,128)S(1)} custom-call(bf16[2,1280,128]{2,1,0:T(8,128)(2,1)} %bitcast.7, bf16[2,1280,1280]{2,1,0:T(8,128)(2,1)} %bitcast.5, bf16[2,512,1280]{2,1,0:T(8,128)(2,1)} %bitcast.6, s32[6,1,192]{2,1,0:T(1,128)} %bitcast.8, s32[1,6]{1,0:T(1,128)} %bitcast.9), custom_call_target="tpu_custom_call" | custom-call | flops 8000000000 | bytes 10000000 | tf_op jit(solution)/shard_map/schwarz/pallas_call | solution.py:370
  41.8 0.6 %copy.7 = f32[2,4,64]{2,1,0:T(4,128)} copy(f32[2,4,64]{2,1,0:T(4,128)S(1)} %schwarz.1) | data formatting | bytes 4096

commit v4 on v3

--- a/solution.py
+++ b/solution.py
@@ -18,7 +18,6 @@
 PART_ROWS = ANG // PARTS
 BLOCK = 64
 MESH = pl.DeviceIdType.MESH
-PICK_ORDER = (4, 0, 1, 2, 3, 5)
 TAKE_ORDER = (2, 0, 1)
 BF16, F32 = jnp.bfloat16, jnp.float32
 
@@ -55,7 +54,6 @@
             load.start()
 
     start_response(0)
-    start_response(1)
     rad_loads = [
         pltpu.make_async_copy(radiation.at[p], rad.at[:, pl.ds(p * M, M)], load_sem.at[3 + p]) for p in range(2)
     ]
@@ -95,6 +93,8 @@
     @pl.when(middle)
     def _():
         greet(cross)
+
+    start_response(1)
 
     ahead, across = core, 1 - core
     face_of = (4 * ahead, 4 * ahead + 1, 4 * across, 4 * across + 1, 2 + core, 3 - core)
@@ -121,14 +121,15 @@
     for f in range(6):
         slots[f : f + 1, 0:FACE] = slots_raw[f]
     lanes128 = lax.broadcasted_iota(jnp.int32, (128, 128), 1).astype(F32)
-    for r in PICK_ORDER:
+    for r in range(6):
         row = slots[pl.ds(face_of[r], 1), :].astype(F32)
         for half, count in ((0, 128), (1, 64)):
             wide = jnp.broadcast_to(row[:, half * 128 : (half + 1) * 128], (128, 128))
             tall = jnp.transpose(wide)[:count]
             for c in range(M // 128):
                 hit = tall - float(c * 128) == lanes128[:count]
-                select[r, half * 128 : half * 128 + count, c * 128 : (c + 1) * 128] = jnp.where(hit, 1.0, 0.0).astype(BF16)
+                start = (r % 2) * FACE + half * 128
+                select[r // 2, start : start + count, c * 128 : (c + 1) * 128] = jnp.where(hit, 1.0, 0.0).astype(BF16)
 
     def set_weights(rows, real, imag):
         low = pl.ds(rows.start, rows.size)
@@ -172,29 +173,24 @@
             device_id_type=MESH,
         )
 
-    crossing = jnp.where((gz == 3) | (gz == 4), 1, 0)
-    far = 2 * across + jnp.where(gz == 3, 1, 0)
-    sequence = [
-        usual + crossing * (other - usual)
-        for usual, other in zip(PICK_ORDER, (far, 4, (far + 1) % 4, (far + 2) % 4, (far + 3) % 4))
-    ]
+    early = across * jnp.where((gz == 3) | (gz == 4), 1, 0)
 
     def send_faces(it):
-        for r in sequence:
-            sent[it, r] = jnp.dot(select[r], outgoing[...], preferred_element_type=F32).astype(BF16)
-            line = jnp.where(r < 4, 1, 0)
-            up = r % 2
-            along_z = (r // 2 + core + 1) % 2 * line
-            along_x = (r // 2 + core) % 2 * line
-            move = 2 * up - 1
-            device = (gx + along_z * move, gy + (1 - line) * (3 - 2 * gy), gz + along_x * move)
+        for g in (early, 1 - early, 2):
+            picked = jnp.dot(select[g], outgoing[...], preferred_element_type=F32).astype(BF16)
+            for up in range(2):
+                sent[it, 2 * g + up] = picked[up * FACE : (up + 1) * FACE]
+            if isinstance(g, int):
+                pl.when(middle)(face_copy(it, 4, 4, cross).start)
+                face_copy(it, 5, 5, partner).start()
+                continue
+            along_x = (g + core) % 2
+            along_z = 1 - along_x
             at = gx * along_z + gz * along_x
-            last = 7 * up
-            inside = ((r < 4) & (at != last)) | ((r == 4) & middle)
-            spot = r + line * (1 - 2 * up)
-            pl.when(inside)(face_copy(it, r, spot, device).start)
-        sent[it, 5] = jnp.dot(select[5], outgoing[...], preferred_element_type=F32).astype(BF16)
-        face_copy(it, 5, 5, partner).start()
+            for up in range(2):
+                move = 2 * up - 1
+                device = (gx + along_z * move, gy, gz + along_x * move)
+                pl.when(at != 7 * up)(face_copy(it, 2 * g + up, 2 * g + 1 - up, device).start)
 
     def take_faces(it, roles):
         for r in roles:
@@ -379,7 +375,7 @@
             pltpu.VMEM((6, 1, FACE), jnp.int32),
             pltpu.VMEM((8, PADDED), jnp.int32),
             pltpu.SMEM((1, 6), jnp.int32),
-            pltpu.VMEM((6, FACE, M), BF16),
+            pltpu.VMEM((3, 2 * FACE, M), BF16),
             pltpu.VMEM((M, 6 * PADDED), BF16),
             pltpu.VMEM((2 * M, 2 * EXC), BF16),
             pltpu.VMEM((M, 2 * EXC), BF16),

time: 42.4 us -> 41.5 us (0.979)
  Pallas kernels: 41.8 us -> 40.8 us
    pallas_call x1, Pallas kernels: 41.8 us -> 40.8 us  [shards(): pl.pallas_call(kernel, out_shape=pltpu.VMEM((2, 4, BLOCK), F32), in_specs...]
where the time goes in v4:
time: 41.5 us; the launch traced here: 41.4 us
  Pallas kernels  40.8 us (98%)
  local copies, waits for them, and re-layouts  0.6 us (1%)
    pallas_call x1, Pallas kernels, shards(): pl.pallas_call(kernel, out_shape=pltpu.VMEM((2, 4, BLOCK), F32), in_specs...  40.8 us

profile of v4, /device:TPU:1, one launch (start us, length us, event | category | flops | bytes accessed | tf_op | source)
XLA Modules:
  0.0 41.4 jit_solution(10838852072336891411)
XLA Ops:
  0.0 40.8 %schwarz.1 = f32[2,4,64]{2,1,0:T(4,128)S(1)} custom-call(bf16[2,1280,128]{2,1,0:T(8,128)(2,1)} %bitcast.7, bf16[2,1280,1280]{2,1,0:T(8,128)(2,1)} %bitcast.5, bf16[2,512,1280]{2,1,0:T(8,128)(2,1)} %bitcast.6, s32[6,1,192]{2,1,0:T(1,128)} %bitcast.8, s32[1,6]{1,0:T(1,128)} %bitcast.9), custom_call_target="tpu_custom_call" | custom-call | flops 8000000000 | bytes 10000000 | tf_op jit(solution)/shard_map/schwarz/pallas_call | solution.py:366
  40.8 0.6 %copy.7 = f32[2,4,64]{2,1,0:T(4,128)} copy(f32[2,4,64]{2,1,0:T(4,128)S(1)} %schwarz.1) | data formatting | bytes 4096

commit v5 on v4

--- a/solution.py
+++ b/solution.py
@@ -12,9 +12,10 @@
 ANG = 512
 EXC = 128
 PADDED = 256
+PAIR = 2 * FACE
 CHUNKS = 5
 ROWS = M // CHUNKS
-PARTS = 4
+PARTS = 2
 PART_ROWS = ANG // PARTS
 BLOCK = 64
 MESH = pl.DeviceIdType.MESH
@@ -29,9 +30,10 @@
 
 def kernel(
     incident, response, radiation, face_index, linked, out_ref,
-    inc, resp, rad, slots_raw, slots, link, select, place, weights, outgoing, sent, near_in, far_in, total, columns, field,
-    keep, half_out, half_in, plane_out, plane_in, line_out, line_in,
-    load_sem, resp_sem, face_send, face_recv, half_send, half_recv, plane_send, plane_recv, line_send, line_recv,
+    inc, resp, rad, slots_raw, slots, link, rows_of, select, place, weights, outgoing, sent, split, near_in, far_in, total,
+    columns, keep, half_out, half_in, plane_out, plane_in, line_out, line_in,
+    load_sem, resp_sem, face_send, face_recv, split_send, split_recv, half_send, half_recv, column_send, column_recv,
+    plane_send, plane_recv, line_send, line_recv,
 ):
     loads = [
         pltpu.make_async_copy(face_index, slots_raw, load_sem.at[0]),
@@ -64,8 +66,9 @@
     me_plane = gz * 2 + y_lo
 
     near_in[...] = jnp.zeros_like(near_in)
-    for g in range(3):
-        far_in[g, 0 : 2 * PADDED] = jnp.zeros((2 * PADDED, 2 * EXC), BF16)
+    for s in range(2):
+        for g in range(3):
+            far_in[s, g, 0:PAIR] = jnp.zeros((PAIR, EXC), BF16)
     plane_in[...] = jnp.zeros_like(plane_in)
     line_in[...] = jnp.zeros_like(line_in)
 
@@ -89,10 +92,10 @@
     for d in range(1, 8):
         greet(((gx + d) % 8, gy, gz))
     greet(partner)
-
-    @pl.when(middle)
-    def _():
-        greet(cross)
+    greet(cross)
+    for d in (1, 7):
+        greet(((gx + d) % 8, gy + 1 - 2 * core, gz))
+        greet((gx, gy + 1 - 2 * core, (gz + d) % 8))
 
     start_response(1)
 
@@ -158,48 +161,89 @@
                         load.start()
             outgoing[rows] = jnp.dot(resp[rows], weights[...], preferred_element_type=F32).astype(BF16)
 
-    def into(it, spot):
-        if it == 0:
-            return near_in.at[pl.ds(spot * PADDED, FACE)]
-        return far_in.at[spot // 2, pl.ds((spot % 2) * PADDED, FACE)]
-
-    def face_copy(it, role, spot, device):
+    def face_copy(role, spot, device):
         return pltpu.make_async_remote_copy(
-            src_ref=sent.at[it, role],
-            dst_ref=into(it, spot),
-            send_sem=face_send.at[it, role],
-            recv_sem=face_recv.at[it, spot],
+            src_ref=sent.at[role],
+            dst_ref=near_in.at[pl.ds(spot * FACE, FACE)],
+            send_sem=face_send.at[role],
+            recv_sem=face_recv.at[spot],
             device_id=device,
             device_id_type=MESH,
         )
 
+    def split_copy(role, half, into, g, up, device):
+        return pltpu.make_async_remote_copy(
+            src_ref=split.at[half, role],
+            dst_ref=far_in.at[into, g, pl.ds(up * FACE, FACE)],
+            send_sem=split_send.at[half, role],
+            recv_sem=split_recv.at[into, 2 * g + up],
+            device_id=device,
+            device_id_type=MESH,
+        )
+
+    def halves(value, rows):
+        odd = (lax.broadcasted_iota(jnp.int32, (rows, EXC), 1) // 4) % 2
+        real, imag = value[:, 0:EXC], value[:, EXC : 2 * EXC]
+        zero = jnp.where(odd == 0, real, pltpu.roll(imag, 4, 1))
+        one = jnp.where(odd == 0, pltpu.roll(real, EXC - 4, 1), imag)
+        return zero, one
+
     early = across * jnp.where((gz == 3) | (gz == 4), 1, 0)
 
     def send_faces(it):
         for g in (early, 1 - early, 2):
-            picked = jnp.dot(select[g], outgoing[...], preferred_element_type=F32).astype(BF16)
-            for up in range(2):
-                sent[it, 2 * g + up] = picked[up * FACE : (up + 1) * FACE]
+            picked = jnp.dot(select[g], outgoing[...], preferred_element_type=F32)
+            if it == 0:
+                rounded = picked.astype(BF16)
+                for up in range(2):
+                    sent[2 * g + up] = rounded[up * FACE : (up + 1) * FACE]
+            else:
+                for half, value in enumerate(halves(picked, PAIR)):
+                    rounded = value.astype(BF16)
+                    for up in range(2):
+                        split[half, 2 * g + up] = rounded[up * FACE : (up + 1) * FACE]
             if isinstance(g, int):
-                pl.when(middle)(face_copy(it, 4, 4, cross).start)
-                face_copy(it, 5, 5, partner).start()
+                if it == 0:
+                    pl.when(middle)(face_copy(4, 4, cross).start)
+                    face_copy(5, 5, partner).start()
+                else:
+                    for half in range(2):
+                        pl.when(middle)(split_copy(4, half, across, 2, 0, (gx, (1 - y_lo) * 2 + half, gz)).start)
+                    split_copy(5, across, across, 2, 1, partner).start()
+                    far_in[across, 2, FACE : 2 * FACE] = split[core, 5]
                 continue
             along_x = (g + core) % 2
             along_z = 1 - along_x
             at = gx * along_z + gz * along_x
             for up in range(2):
                 move = 2 * up - 1
-                device = (gx + along_z * move, gy, gz + along_x * move)
-                pl.when(at != 7 * up)(face_copy(it, 2 * g + up, 2 * g + 1 - up, device).start)
-
-    def take_faces(it, roles):
+                inside = at != 7 * up
+                if it == 0:
+                    device = (gx + along_z * move, gy, gz + along_x * move)
+                    pl.when(inside)(face_copy(2 * g + up, 2 * g + 1 - up, device).start)
+                    continue
+                for half in range(2):
+                    device = (gx + along_z * move, y_lo * 2 + half, gz + along_x * move)
+                    pl.when(inside)(split_copy(2 * g + up, half, core, g, 1 - up, device).start)
+
+    def take_faces(roles):
         for r in roles:
-            guarded(r, face_copy(it, r, r, target[r]).wait_recv)
+            guarded(r, face_copy(r, r, target[r]).wait_recv)
+
+    def take_halves(g):
+        for s in range(2):
+            for up in range(2):
+                wait = split_copy(2 * g + up, 0, s, g, up, partner).wait_recv
+                if g == 2:
+                    pl.when(s == core if up else s != y_lo)(wait)
+                else:
+                    spot = gx if (g + s) % 2 == 0 else gz
+                    pl.when(spot < 7 if up else spot > 0)(wait)
 
     def add_traces():
         for n, g in enumerate(TAKE_ORDER):
-            take_faces(0, (2 * g, 2 * g + 1))
-            span = slice(2 * g * PADDED, (2 * g + 2) * PADDED)
+            take_faces((2 * g, 2 * g + 1))
+            span = slice(g * PAIR, (g + 1) * PAIR)
             for c in range(CHUNKS):
                 rows = pl.ds(c * ROWS, ROWS)
                 trace = jnp.dot(place[rows, span], near_in[span], preferred_element_type=F32)
@@ -212,55 +256,38 @@
                     imag = (trace[:, EXC : 2 * EXC] + inc[1, rows].astype(F32)).astype(BF16)
                     set_weights(rows, real, imag)
 
-    def gather_columns(g, p):
-        picked = jnp.dot(
-            rad[:, p * M : (p + 1) * M], place[:, 2 * g * PADDED : (2 * g + 2) * PADDED], preferred_element_type=F32
+    def column_copy(s, g):
+        return pltpu.make_async_remote_copy(
+            src_ref=columns.at[s, g],
+            dst_ref=columns.at[s, g],
+            send_sem=column_send.at[g],
+            recv_sem=column_recv.at[g],
+            device_id=partner,
+            device_id_type=MESH,
         )
-        columns[g, :, 2 * p * PADDED : (2 * p + 2) * PADDED] = picked.astype(BF16)
+
+    def gather_columns(g):
+        for p in range(2):
+            picked = jnp.dot(
+                rad[:, p * M : (p + 1) * M], place[:, g * PAIR : (g + 1) * PAIR], preferred_element_type=F32
+            )
+            columns[core, g, :, p * PAIR : (p + 1) * PAIR] = picked.astype(BF16)
+        column_copy(core, g).start()
 
     respond(True)
-    pl.semaphore_wait(barrier, 15 + 7 + 1 + jnp.where(middle, 1, 0))
+    pl.semaphore_wait(barrier, 15 + 7 + 2 + 4)
     send_faces(0)
 
     for load in rad_loads:
         load.wait()
-    field[...] = jnp.dot(rad[...], weights[...], preferred_element_type=F32)
-    loads[2].wait()
-    for r in range(6):
-        row = jnp.where(link[0, face_of[r]] > 0, slots[pl.ds(face_of[r], 1), :], -1)
-        for c in range(CHUNKS):
-            spots = lax.broadcasted_iota(jnp.int32, (ROWS, PADDED), 0) + c * ROWS
-            place[c * ROWS : (c + 1) * ROWS, r * PADDED : (r + 1) * PADDED] = jnp.where(spots == row, 1.0, 0.0).astype(BF16)
-    gather_columns(TAKE_ORDER[0], 0)
-    gather_columns(TAKE_ORDER[0], 1)
-
-    add_traces()
-    respond(False)
-    send_faces(1)
-    for g in TAKE_ORDER[1:]:
-        gather_columns(g, 0)
-        gather_columns(g, 1)
-
-    lanes = lax.broadcasted_iota(jnp.int32, (PART_ROWS, EXC), 1)
-    odd_core = (lanes // 4) % 2
     half_copies = []
-    for n, g in enumerate(TAKE_ORDER):
-        take_faces(1, (2 * g, 2 * g + 1))
-        low, high = slice(0, 2 * PADDED), slice(2 * PADDED, 4 * PADDED)
-        far_in[g, high, 0:EXC] = -far_in[g, low, EXC : 2 * EXC]
-        far_in[g, high, EXC : 2 * EXC] = far_in[g, low, 0:EXC]
-        for q in range(PARTS):
-            rows = pl.ds(q * PART_ROWS, PART_ROWS)
-            value = field[rows] + jnp.dot(columns[g, rows], far_in[g], preferred_element_type=F32)
-            if n < 2:
-                field[rows] = value
-                continue
-            real, imag = value[:, 0:EXC], value[:, EXC : 2 * EXC]
-            zero = jnp.where(odd_core == 0, real, pltpu.roll(imag, 4, 1))
-            one = jnp.where(odd_core == 0, pltpu.roll(real, EXC - 4, 1), imag)
-            keep[rows] = jnp.where(core == 0, zero, one)
-            half_out[rows] = jnp.where(core == 0, one, zero)
-            copy = pltpu.make_async_remote_copy(
+    for q in range(PARTS):
+        rows = pl.ds(q * PART_ROWS, PART_ROWS)
+        zero, one = halves(jnp.dot(rad[rows], weights[...], preferred_element_type=F32), PART_ROWS)
+        keep[rows] = jnp.where(core == 0, zero, one)
+        half_out[rows] = jnp.where(core == 0, one, zero)
+        half_copies.append(
+            pltpu.make_async_remote_copy(
                 src_ref=half_out.at[rows],
                 dst_ref=half_in.at[rows],
                 send_sem=half_send.at[q],
@@ -268,22 +295,53 @@
                 device_id=partner,
                 device_id_type=MESH,
             )
-            copy.start()
-            half_copies.append(copy)
-
+        )
+        half_copies[q].start()
+    loads[2].wait()
+    for r in range(6):
+        row = jnp.where(link[0, face_of[r]] > 0, slots_raw[face_of[r]], -1)
+        rows_of[r // 2 : r // 2 + 1, (r % 2) * FACE : (r % 2 + 1) * FACE] = row
+    for g in range(3):
+        row = rows_of[g : g + 1, :]
+        for c in range(CHUNKS):
+            spots = lax.broadcasted_iota(jnp.int32, (ROWS, PAIR), 0) + c * ROWS
+            place[c * ROWS : (c + 1) * ROWS, g * PAIR : (g + 1) * PAIR] = jnp.where(spots == row, 1.0, 0.0).astype(BF16)
+    gather_columns(TAKE_ORDER[0])
+
+    add_traces()
+    respond(False)
+    send_faces(1)
+    for g in TAKE_ORDER[1:]:
+        gather_columns(g)
+
+    odd_part = (lax.broadcasted_iota(jnp.int32, (PAIR, EXC), 1) // 4) % 2
     small = lax.broadcasted_iota(jnp.int32, (BLOCK // 2, EXC), 1)
     odd_lo = (small // 8) % 2
-    for q in range(PARTS):
-        half_copies[q].wait_recv()
-        for b in range(PART_ROWS // BLOCK):
-            start = q * PART_ROWS + b * BLOCK
-            first = pl.ds(start, BLOCK // 2)
-            second = pl.ds(start + BLOCK // 2, BLOCK // 2)
-            top = keep[first] + half_in[first]
-            low = keep[second] + half_in[second]
-            slot = (q * (PART_ROWS // BLOCK) + b) * 2
-            plane_out[slot] = jnp.where(odd_lo == 0, top, pltpu.roll(low, 8, 1)).astype(BF16)
-            plane_out[slot + 1] = jnp.where(odd_lo == 0, pltpu.roll(top, EXC - 8, 1), low).astype(BF16)
+    for copy in half_copies:
+        copy.wait_recv()
+    for n, g in enumerate(TAKE_ORDER):
+        column_copy(across, g).wait_recv()
+        take_halves(g)
+        for s in range(2):
+            faces = far_in[s, g, 0:PAIR].astype(F32)
+            turned = jnp.where(odd_part == 0, -pltpu.roll(faces, EXC - 4, 1), pltpu.roll(faces, 4, 1))
+            far_in[s, g, PAIR : 2 * PAIR] = turned.astype(BF16)
+        for q in range(PARTS):
+            rows = pl.ds(q * PART_ROWS, PART_ROWS)
+            value = keep[rows]
+            if n == 0:
+                value = value + half_in[rows]
+            for s in range(2):
+                value = value + jnp.dot(columns[s, g, rows], far_in[s, g], preferred_element_type=F32)
+            if n < 2:
+                keep[rows] = value
+                continue
+            for b in range(PART_ROWS // BLOCK):
+                top = value[b * BLOCK : b * BLOCK + BLOCK // 2]
+                low = value[b * BLOCK + BLOCK // 2 : (b + 1) * BLOCK]
+                slot = (q * (PART_ROWS // BLOCK) + b) * 2
+                plane_out[slot] = jnp.where(odd_lo == 0, top, pltpu.roll(low, 8, 1)).astype(BF16)
+                plane_out[slot + 1] = jnp.where(odd_lo == 0, pltpu.roll(top, EXC - 8, 1), low).astype(BF16)
 
     plane_copies = []
     for n, step in enumerate(order):
@@ -332,9 +390,14 @@
         copy.start()
         line_copies.append(copy)
 
-    for it in range(2):
-        for r in range(6):
-            guarded(r, face_copy(it, r, landing[r], target[r]).wait_send)
+    for r in range(6):
+        guarded(r, face_copy(r, landing[r], target[r]).wait_send)
+        for half in range(2):
+            if r < 5:
+                guarded(r, split_copy(r, half, 0, 0, 0, target[r]).wait_send)
+    split_copy(5, across, 0, 0, 0, partner).wait_send()
+    for g in range(3):
+        column_copy(core, g).wait_send()
     for copy in half_copies + plane_copies:
         copy.wait_send()
 
@@ -375,16 +438,17 @@
             pltpu.VMEM((6, 1, FACE), jnp.int32),
             pltpu.VMEM((8, PADDED), jnp.int32),
             pltpu.SMEM((1, 6), jnp.int32),
-            pltpu.VMEM((3, 2 * FACE, M), BF16),
-            pltpu.VMEM((M, 6 * PADDED), BF16),
+            pltpu.VMEM((8, PAIR), jnp.int32),
+            pltpu.VMEM((3, PAIR, M), BF16),
+            pltpu.VMEM((M, 3 * PAIR), BF16),
             pltpu.VMEM((2 * M, 2 * EXC), BF16),
             pltpu.VMEM((M, 2 * EXC), BF16),
-            pltpu.VMEM((2, 6, FACE, 2 * EXC), BF16),
-            pltpu.VMEM((6 * PADDED, 2 * EXC), BF16),
-            pltpu.VMEM((3, 4 * PADDED, 2 * EXC), BF16),
+            pltpu.VMEM((6, FACE, 2 * EXC), BF16),
+            pltpu.VMEM((2, 6, FACE, EXC), BF16),
+            pltpu.VMEM((3 * PAIR, 2 * EXC), BF16),
+            pltpu.VMEM((2, 3, 2 * PAIR, EXC), BF16),
             pltpu.VMEM((M, 2 * EXC), F32),
-            pltpu.VMEM((3, ANG, 4 * PADDED), BF16),
-            pltpu.VMEM((ANG, 2 * EXC), F32),
+            pltpu.VMEM((2, 3, ANG, 2 * PAIR), BF16),
             pltpu.VMEM((ANG, EXC), F32),
             pltpu.VMEM((ANG, EXC), F32),
             pltpu.VMEM((ANG, EXC), F32),
@@ -394,10 +458,14 @@
             pltpu.VMEM((8, 8, EXC), F32),
             dma((5,)),
             dma((CHUNKS, 2)),
+            dma((6,)),
+            dma((6,)),
             dma((2, 6)),
             dma((2, 6)),
             dma((PARTS,)),
             dma((PARTS,)),
+            dma((3,)),
+            dma((3,)),
             dma((16,)),
             dma((16,)),
             dma((8,)),

time: 41.5 us -> 41.6 us (level)
  no operation moved by 1% of the time
where the time goes in v5:
time: 41.6 us; the launch traced here: 41.5 us
  Pallas kernels  40.8 us (98%)
  local copies, waits for them, and re-layouts  0.6 us (1%)
    pallas_call x1, Pallas kernels, shards(): pl.pallas_call(kernel, out_shape=pltpu.VMEM((2, 4, BLOCK), F32), in_specs...  40.8 us

profile of v5, /device:TPU:1, one launch (start us, length us, event | category | flops | bytes accessed | tf_op | source)
XLA Modules:
  0.0 41.5 jit_solution(13073148033509249456)
XLA Ops:
  0.0 40.8 %schwarz.1 = f32[2,4,64]{2,1,0:T(4,128)S(1)} custom-call(bf16[2,1280,128]{2,1,0:T(8,128)(2,1)} %bitcast.7, bf16[2,1280,1280]{2,1,0:T(8,128)(2,1)} %bitcast.5, bf16[2,512,1280]{2,1,0:T(8,128)(2,1)} %bitcast.6, s32[6,1,192]{2,1,0:T(1,128)} %bitcast.8, s32[1,6]{1,0:T(1,128)} %bitcast.9), custom_call_target="tpu_custom_call" | custom-call | flops 8000000000 | bytes 10000000 | tf_op jit(solution)/shard_map/schwarz/pallas_call | solution.py:429
  40.9 0.6 %copy.7 = f32[2,4,64]{2,1,0:T(4,128)} copy(f32[2,4,64]{2,1,0:T(4,128)S(1)} %schwarz.1) | data formatting | bytes 4096

commit v6 on v5

--- a/solution.py
+++ b/solution.py
@@ -19,7 +19,7 @@
 PART_ROWS = ANG // PARTS
 BLOCK = 64
 MESH = pl.DeviceIdType.MESH
-TAKE_ORDER = (2, 0, 1)
+TAKE_ORDER = (0, 2, 1)
 BF16, F32 = jnp.bfloat16, jnp.float32
 
 
@@ -317,6 +317,7 @@
     odd_part = (lax.broadcasted_iota(jnp.int32, (PAIR, EXC), 1) // 4) % 2
     small = lax.broadcasted_iota(jnp.int32, (BLOCK // 2, EXC), 1)
     odd_lo = (small // 8) % 2
+    plane_copies = []
     for copy in half_copies:
         copy.wait_recv()
     for n, g in enumerate(TAKE_ORDER):
@@ -327,7 +328,8 @@
             turned = jnp.where(odd_part == 0, -pltpu.roll(faces, EXC - 4, 1), pltpu.roll(faces, 4, 1))
             far_in[s, g, PAIR : 2 * PAIR] = turned.astype(BF16)
         for q in range(PARTS):
-            rows = pl.ds(q * PART_ROWS, PART_ROWS)
+            part = q if n < 2 else (1 - y_hi if q == 0 else y_hi)
+            rows = pl.ds(pl.multiple_of(part * PART_ROWS, PART_ROWS), PART_ROWS)
             value = keep[rows]
             if n == 0:
                 value = value + half_in[rows]
@@ -339,23 +341,24 @@
             for b in range(PART_ROWS // BLOCK):
                 top = value[b * BLOCK : b * BLOCK + BLOCK // 2]
                 low = value[b * BLOCK + BLOCK // 2 : (b + 1) * BLOCK]
-                slot = (q * (PART_ROWS // BLOCK) + b) * 2
+                slot = (part * (PART_ROWS // BLOCK) + b) * 2
                 plane_out[slot] = jnp.where(odd_lo == 0, top, pltpu.roll(low, 8, 1)).astype(BF16)
                 plane_out[slot + 1] = jnp.where(odd_lo == 0, pltpu.roll(top, EXC - 8, 1), low).astype(BF16)
-
-    plane_copies = []
-    for n, step in enumerate(order):
-        peer, device = plane_peer(step)
-        copy = pltpu.make_async_remote_copy(
-            src_ref=plane_out.at[peer],
-            dst_ref=plane_in.at[me_plane],
-            send_sem=plane_send.at[n],
-            recv_sem=plane_recv.at[me_plane],
-            device_id=device,
-            device_id_type=MESH,
-        )
-        copy.start()
-        plane_copies.append(copy)
+            for k, step in enumerate(order):
+                if step[0] == q:
+                    continue
+                peer, device = plane_peer(step)
+                copy = pltpu.make_async_remote_copy(
+                    src_ref=plane_out.at[peer],
+                    dst_ref=plane_in.at[me_plane],
+                    send_sem=plane_send.at[k],
+                    recv_sem=plane_recv.at[me_plane],
+                    device_id=device,
+                    device_id_type=MESH,
+                )
+                copy.start()
+                plane_copies.append(copy)
+
     for s in range(16):
 
         @pl.when(s != me_plane)

time: 41.6 us -> 41.1 us (0.988)
    pallas_call x1, Pallas kernels: 40.8 us -> 40.4 us  [shards(): pl.pallas_call(kernel, out_shape=pltpu.VMEM((2, 4, BLOCK), F32), in_specs...]
where the time goes in v6:
time: 41.1 us; the launch traced here: 41 us
  Pallas kernels  40.4 us (98%)
  local copies, waits for them, and re-layouts  0.6 us (1%)
    pallas_call x1, Pallas kernels, shards(): pl.pallas_call(kernel, out_shape=pltpu.VMEM((2, 4, BLOCK), F32), in_specs...  40.4 us

profile of v6, /device:TPU:1, one launch (start us, length us, event | category | flops | bytes accessed | tf_op | source)
XLA Modules:
  0.0 41.0 jit_solution(5386475813739630199)
XLA Ops:
  0.0 40.4 %schwarz.1 = f32[2,4,64]{2,1,0:T(4,128)S(1)} custom-call(bf16[2,1280,128]{2,1,0:T(8,128)(2,1)} %bitcast.7, bf16[2,1280,1280]{2,1,0:T(8,128)(2,1)} %bitcast.5, bf16[2,512,1280]{2,1,0:T(8,128)(2,1)} %bitcast.6, s32[6,1,192]{2,1,0:T(1,128)} %bitcast.8, s32[1,6]{1,0:T(1,128)} %bitcast.9), custom_call_target="tpu_custom_call" | custom-call | flops 8000000000 | bytes 10000000 | tf_op jit(solution)/shard_map/schwarz/pallas_call | solution.py:432
  40.4 0.6 %copy.7 = f32[2,4,64]{2,1,0:T(4,128)} copy(f32[2,4,64]{2,1,0:T(4,128)S(1)} %schwarz.1) | data formatting | bytes 4096

commit v7 on v4

--- a/solution.py
+++ b/solution.py
@@ -18,7 +18,7 @@
 PART_ROWS = ANG // PARTS
 BLOCK = 64
 MESH = pl.DeviceIdType.MESH
-TAKE_ORDER = (2, 0, 1)
+TAKE_ORDER = (0, 2, 1)
 BF16, F32 = jnp.bfloat16, jnp.float32
 
 
@@ -244,13 +244,15 @@
     lanes = lax.broadcasted_iota(jnp.int32, (PART_ROWS, EXC), 1)
     odd_core = (lanes // 4) % 2
     half_copies = []
+    parts = [(1 - y_hi) * 2, (1 - y_hi) * 2 + 1, y_hi * 2, y_hi * 2 + 1]
     for n, g in enumerate(TAKE_ORDER):
         take_faces(1, (2 * g, 2 * g + 1))
         low, high = slice(0, 2 * PADDED), slice(2 * PADDED, 4 * PADDED)
         far_in[g, high, 0:EXC] = -far_in[g, low, EXC : 2 * EXC]
         far_in[g, high, EXC : 2 * EXC] = far_in[g, low, 0:EXC]
         for q in range(PARTS):
-            rows = pl.ds(q * PART_ROWS, PART_ROWS)
+            part = q if n < 2 else parts[q]
+            rows = pl.ds(pl.multiple_of(part * PART_ROWS, PART_ROWS), PART_ROWS)
             value = field[rows] + jnp.dot(columns[g, rows], far_in[g], preferred_element_type=F32)
             if n < 2:
                 field[rows] = value
@@ -273,31 +275,35 @@
 
     small = lax.broadcasted_iota(jnp.int32, (BLOCK // 2, EXC), 1)
     odd_lo = (small // 8) % 2
+    plane_copies = []
     for q in range(PARTS):
         half_copies[q].wait_recv()
         for b in range(PART_ROWS // BLOCK):
-            start = q * PART_ROWS + b * BLOCK
-            first = pl.ds(start, BLOCK // 2)
-            second = pl.ds(start + BLOCK // 2, BLOCK // 2)
+            start = parts[q] * PART_ROWS + b * BLOCK
+            first = pl.ds(pl.multiple_of(start, BLOCK // 2), BLOCK // 2)
+            second = pl.ds(pl.multiple_of(start + BLOCK // 2, BLOCK // 2), BLOCK // 2)
             top = keep[first] + half_in[first]
             low = keep[second] + half_in[second]
-            slot = (q * (PART_ROWS // BLOCK) + b) * 2
+            slot = (parts[q] * (PART_ROWS // BLOCK) + b) * 2
             plane_out[slot] = jnp.where(odd_lo == 0, top, pltpu.roll(low, 8, 1)).astype(BF16)
             plane_out[slot + 1] = jnp.where(odd_lo == 0, pltpu.roll(top, EXC - 8, 1), low).astype(BF16)
-
-    plane_copies = []
-    for n, step in enumerate(order):
-        peer, device = plane_peer(step)
-        copy = pltpu.make_async_remote_copy(
-            src_ref=plane_out.at[peer],
-            dst_ref=plane_in.at[me_plane],
-            send_sem=plane_send.at[n],
-            recv_sem=plane_recv.at[me_plane],
-            device_id=device,
-            device_id_type=MESH,
-        )
-        copy.start()
-        plane_copies.append(copy)
+        if q % 2 == 0:
+            continue
+        for k, step in enumerate(order):
+            if step[0] == q // 2:
+                continue
+            peer, device = plane_peer(step)
+            copy = pltpu.make_async_remote_copy(
+                src_ref=plane_out.at[peer],
+                dst_ref=plane_in.at[me_plane],
+                send_sem=plane_send.at[k],
+                recv_sem=plane_recv.at[me_plane],
+                device_id=device,
+                device_id_type=MESH,
+            )
+            copy.start()
+            plane_copies.append(copy)
+
     for s in range(16):
 
         @pl.when(s != me_plane)

time: 41.5 us -> 40.3 us (0.971)
  Pallas kernels: 40.8 us -> 39.6 us
    pallas_call x1, Pallas kernels: 40.8 us -> 39.6 us  [shards(): pl.pallas_call(kernel, out_shape=pltpu.VMEM((2, 4, BLOCK), F32), in_specs...]
where the time goes in v7:
time: 40.3 us; the launch traced here: 40.2 us
  Pallas kernels  39.6 us (98%)
  local copies, waits for them, and re-layouts  0.6 us (1%)
    pallas_call x1, Pallas kernels, shards(): pl.pallas_call(kernel, out_shape=pltpu.VMEM((2, 4, BLOCK), F32), in_specs...  39.6 us

profile of v7, /device:TPU:1, one launch (start us, length us, event | category | flops | bytes accessed | tf_op | source)
XLA Modules:
  0.0 40.2 jit_solution(18217645560994135072)
XLA Ops:
  0.0 39.6 %schwarz.1 = f32[2,4,64]{2,1,0:T(4,128)S(1)} custom-call(bf16[2,1280,128]{2,1,0:T(8,128)(2,1)} %bitcast.7, bf16[2,1280,1280]{2,1,0:T(8,128)(2,1)} %bitcast.5, bf16[2,512,1280]{2,1,0:T(8,128)(2,1)} %bitcast.6, s32[6,1,192]{2,1,0:T(1,128)} %bitcast.8, s32[1,6]{1,0:T(1,128)} %bitcast.9), custom_call_target="tpu_custom_call" | custom-call | flops 8000000000 | bytes 10000000 | tf_op jit(solution)/shard_map/schwarz/pallas_call | solution.py:372
  39.6 0.6 %copy.7 = f32[2,4,64]{2,1,0:T(4,128)} copy(f32[2,4,64]{2,1,0:T(4,128)S(1)} %schwarz.1) | data formatting | bytes 4096
